TPU v7x, 8 devices: a whole 2x2x1 slice. The times are simulated.
8 devices in a mesh: model: 2 (over z, y), sub: 2 (over x), data: 2 (over core).
Axes of the slice: x: 2, y: 2, z: 1, core: 2. Of those that a mesh axis runs over, the one named last changes fastest.
Arguments:
- images: bfloat16 [24, 576, 768], P(('model', 'sub', 'data'))
- targets: bfloat16 [24, 576, 768], P(('model', 'sub', 'data'))
- w_in: float32 [6, 768, 3072], replicated
- w_out: float32 [6, 3072, 768], replicated
Outputs:
- output 1: float32 [6, 768, 3072], replicated
- output 2: float32 [6, 3072, 768], replicated
- output 3: float32 [], replicated
All inputs are finite; a program needn't handle non-finite values.
Results may differ from a plain program's by a relative error of at most 0.00469329.
Values are sent between devices in bfloat16 or wider.
A program may use at most 1 GiB of HBM per device.

v0:
```python
import jax
import jax.numpy as jnp
import math
from jax import lax
from jax.sharding import PartitionSpec as P

RHO_REL = 0.1
LEARN_RATE = 8.0
SQRT_HALF = 0.7071067811865476
INV_SQRT_2PI = 0.3989422804014327


def gelu_fn(pre_act):
    return 0.5 * pre_act * (1.0 + lax.erf(pre_act * SQRT_HALF))


def gelu_slope(pre_act):
    cdf_part = 0.5 * (1.0 + lax.erf(pre_act * SQRT_HALF))
    return cdf_part + pre_act * INV_SQRT_2PI * jnp.exp(-0.5 * pre_act * pre_act)


def forward(x_rows, in_list, out_list):
    hidden = x_rows
    saved_acts = []
    for layer_idx in range(len(in_list)):
        pre_act = jnp.dot(hidden, in_list[layer_idx], preferred_element_type=jnp.float32).astype(jnp.bfloat16)
        post_act = gelu_fn(pre_act.astype(jnp.float32)).astype(jnp.bfloat16)
        mlp_out = jnp.dot(post_act, out_list[layer_idx], preferred_element_type=jnp.float32)
        saved_acts.append((hidden, pre_act, post_act))
        hidden = (hidden.astype(jnp.float32) + mlp_out).astype(jnp.bfloat16)
    return hidden, saved_acts


def backward(d_top, saved_acts, in_list, out_list):
    d_hidden = d_top
    grads_in = []
    grads_out = []
    for layer_idx in reversed(range(len(saved_acts))):
        hidden, pre_act, post_act = saved_acts[layer_idx]
        grads_out.append(jnp.einsum('tf,td->fd', post_act, d_hidden, preferred_element_type=jnp.float32))
        d_act = jnp.einsum('td,fd->tf', d_hidden, out_list[layer_idx], preferred_element_type=jnp.float32)
        d_pre = (d_act * gelu_slope(pre_act.astype(jnp.float32))).astype(jnp.bfloat16)
        grads_in.append(jnp.einsum('td,tf->df', hidden, d_pre, preferred_element_type=jnp.float32))
        if layer_idx > 0:
            back_part = jnp.einsum('tf,df->td', d_pre, in_list[layer_idx], preferred_element_type=jnp.float32)
            d_hidden = (d_hidden.astype(jnp.float32) + back_part).astype(jnp.bfloat16)
    return grads_in[::-1], grads_out[::-1]


def top_grad(top_hidden, y_rows, inv_count):
    resid_err = top_hidden.astype(jnp.float32) - y_rows.astype(jnp.float32)
    return 0.5 * jnp.sum(resid_err * resid_err), (resid_err * inv_count).astype(jnp.bfloat16)


def solution(mesh):
    mesh_axes = tuple(mesh.axis_names)
    dev_count = math.prod([mesh.shape[axis_name] for axis_name in mesh_axes])
    batch_spec = P(mesh_axes, None, None)

    def local_step(images, targets, w_in, w_out):
        layers, model_dim, hidden_dim = w_in.shape
        tok_local = images.shape[0] * images.shape[1]
        inv_count = 1.0 / (tok_local * dev_count * model_dim)
        radius = RHO_REL * math.sqrt(layers * hidden_dim + model_dim)
        x_rows = images.reshape(tok_local, model_dim)
        y_rows = targets.reshape(tok_local, model_dim)
        w_in_bf = w_in.astype(jnp.bfloat16)
        w_out_bf = w_out.astype(jnp.bfloat16)
        in_list = [w_in_bf[layer_idx] for layer_idx in range(layers)]
        out_list = [w_out_bf[layer_idx] for layer_idx in range(layers)]
        top_hidden, saved_acts = forward(x_rows, in_list, out_list)
        _, d_top = top_grad(top_hidden, y_rows, inv_count)
        grads_in, grads_out = backward(d_top, saved_acts, in_list, out_list)
        grads_in, grads_out = lax.psum((grads_in, grads_out), mesh_axes)
        norm_sq = sum(jnp.sum(grad_part * grad_part) for grad_part in grads_in + grads_out)
        step_scale = radius / jnp.sqrt(norm_sq)
        pert_in = [(w_in[layer_idx] + step_scale * grads_in[layer_idx]).astype(jnp.bfloat16) for layer_idx in range(layers)]
        pert_out = [(w_out[layer_idx] + step_scale * grads_out[layer_idx]).astype(jnp.bfloat16) for layer_idx in range(layers)]
        top_pert, saved_pert = forward(x_rows, pert_in, pert_out)
        loss_local, d_pert = top_grad(top_pert, y_rows, inv_count)
        grads2_in, grads2_out = backward(d_pert, saved_pert, pert_in, pert_out)
        grads2_in, grads2_out, loss_total = lax.psum((grads2_in, grads2_out, loss_local), mesh_axes)
        new_in = w_in - LEARN_RATE * jnp.stack(grads2_in)
        new_out = w_out - LEARN_RATE * jnp.stack(grads2_out)
        return new_in, new_out, loss_total * inv_count

    return jax.shard_map(local_step, mesh=mesh, in_specs=(batch_spec, batch_spec, P(), P()), out_specs=(P(), P(), P()), check_vma=False)
```

profile of v0, /device:TPU:0, one launch (start us, length us, event | category | flops | bytes accessed | tf_op | source)
XLA Modules:
  0.0 4137.9 jit_solution(11475870034465451221)
XLA Ops:
  7.2 27.5 convert_element_type.356
  34.7 27.7 convert_element_type.352
  62.4 15.1 fusion.8
  77.4 16.8 fusion.136
  94.2 16.1 fusion.17
  110.3 16.8 add_convert_fusion.19
  127.1 16.4 fusion.26
  143.5 16.8 add_convert_fusion.18
  160.3 16.2 fusion.35
  176.5 16.8 add_convert_fusion.17
  193.3 16.6 fusion.44
  209.8 17.0 add_convert_fusion.16
  226.8 16.0 fusion.53
  242.9 18.8 fusion.139
  261.7 22.4 fusion.171
  284.1 21.4 fusion.57
  330.2 17.6 fusion.174
  347.8 21.8 fusion.48
  394.0 17.4 fusion.177
  411.5 21.6 fusion.39
  457.7 17.4 fusion.180
  475.1 21.9 fusion.30
  521.9 17.5 fusion.183
  539.4 21.5 fusion.21
  574.7 31.3 fusion.135
  606.0 18.0 fusion.186
  624.0 14.0 fusion.189
  638.1 55.0 %copy.23 = f32[6,768,3072]{1,2,0:T(8,128)} copy(f32[6,768,3072]{2,1,0:T(8,128)} %param.6) | data formatting | bytes 113246208 | tf_op args[2]
  693.1 1193.5 %all-reduce.7.cloned.1.call-done = (f32[768,3072]{0,1:T(8,128)}, f32[768,3072]{0,1:T(8,128)}, f32[768,3072]{0,1:T(8,128)}, f32[768,3072]{0,1:T(8,128)}, f32[768,...) async-done(((f32[768,3072]{0,1:T(8,128)}, ...) | async-done | bytes 113246224 | tf_op jit(solution)/shard_map/psum | solution.py:74
  1951.1 45.7 %fusion.128 = (bf16[3072,768]{1,0:T(8,128)(2,1)}, bf16[3072,768]{1,0:T(8,128)(2,1)}, bf16[3072,768]{1,0:T(8,128)(2,1)}, bf16[3072,768]{1,0:T(8,128)(2,1)}, bf16[...) fusion(f32[3072,768]{1,0:T(8,128)} %get-tuple-element.29, f32[6,3072,768]{2,1,0:T(8,128)} %param.7, f32[]{:T(128)S(6)} %div.3, ...), kind=kLoop, calls=%fused_computation.208 | loop fusion | flops 42467328 | bytes 141557760 | tf_op jit(solution)/shard_map/convert_element_type | solution.py:78
  1996.9 37.8 fusion.117
  2034.7 21.7 fusion.107
  2056.3 17.2 fusion.137
  2073.6 15.9 fusion.62
  2089.5 18.6 add_convert_fusion.9
  2108.1 16.1 fusion.71
  2124.2 17.0 add_convert_fusion.8
  2141.3 16.0 fusion.80
  2157.3 18.6 add_convert_fusion.7
  2176.0 16.1 fusion.89
  2192.1 17.0 add_convert_fusion.6
  2209.1 16.0 fusion.98
  2225.1 20.2 multiply_reduce_fusion.12
  2245.3 24.5 fusion.102
  2269.8 17.9 convolution_bitcast_fusion.5
  2301.2 16.9 convolution_bitcast_fusion
  2318.2 20.9 fusion.93
  2339.1 18.1 convolution_bitcast_fusion.6
  2370.7 17.1 convolution_bitcast_fusion.1
  2387.9 21.0 fusion.84
  2408.8 18.5 convolution_bitcast_fusion.7
  2440.6 17.0 convolution_bitcast_fusion.2
  2457.6 21.2 fusion.75
  2478.8 18.2 convolution_bitcast_fusion.8
  2510.6 17.1 convolution_bitcast_fusion.3
  2527.8 21.1 fusion.66
  2548.8 18.4 convolution_bitcast_fusion.9
  2592.7 30.8 fusion.134
  2623.5 18.1 convolution_bitcast_fusion.10
  2642.3 23.4 psum.199
  2666.4 1223.0 %all-reduce.5.cloned.1.call-done = (f32[1,768,3072]{1,2,0:T(8,128)}, f32[1,768,3072]{1,2,0:T(8,128)}, f32[1,768,3072]{1,2,0:T(8,128)}, f32[1,768,3072]{1,2,0:T(8...) async-done(((f32[1,768,3072]{1,2,0:T(8,128)}, ...) | async-done | bytes 113246224 | tf_op jit(solution)/shard_map/psum | solution.py:82
  3927.1 54.9 %multiply_subtract_fusion.1 = f32[6,768,3072]{1,2,0:T(8,128)} fusion(f32[6,768,3072]{1,2,0:T(8,128)} %copy.23, f32[6,768,3072]{1,2,0:T(8,128)} %constant_dynamic-update-slice_fusion), kind=kLoop, calls=%fused_computation.1 | loop fusion | flops 28311552 | bytes 169869312 | tf_op jit(solution)/shard_map/sub | solution.py:83
  3982.0 54.9 %copy.24 = f32[6,768,3072]{2,1,0:T(8,128)} copy(f32[6,768,3072]{1,2,0:T(8,128)} %multiply_subtract_fusion.1) | data formatting | bytes 113246208
  4074.6 54.9 %multiply_subtract_fusion = f32[6,3072,768]{2,1,0:T(8,128)} fusion(f32[6,3072,768]{2,1,0:T(8,128)} %param.7, f32[6,3072,768]{2,1,0:T(8,128)} %constant_dynamic-update-slice_fusion.6), kind=kLoop, calls=%fused_computation | loop fusion | flops 28311552 | bytes 169869312 | tf_op jit(solution)/shard_map/sub | solution.py:84
  (214 shorter events, 323.9 us)
Async XLA Ops:
  7.2 1879.5 %all-reduce.7.cloned.1.call-start = ((), (), s32[]{:S(2)}) async-start(), calls=%async_computation.1 | async-start | bytes 226492416 | tf_op jit(solution)/shard_map/psum | solution.py:74
  34.7 27.7 copy-start.2
  94.2 16.1 copy-start.18
  127.1 16.4 copy-start.20
  160.3 16.2 copy-start.22
  193.3 16.6 copy-start.24
  226.8 16.0 copy-start.1
  261.7 22.4 copy-start.6
  305.5 12.7 copy-start.12
  305.6 12.7 copy-start.16
  369.6 12.7 copy-start.13
  369.6 12.7 copy-start.25
  433.0 12.7 copy-start.14
  433.0 12.7 copy-start.23
  445.8 29.3 copy-start.5
  497.0 13.1 copy-start.15
  497.0 13.1 copy-start.21
  560.9 13.8 copy-start.3
  606.0 18.0 copy-start.19
  638.0 3251.3 %all-reduce.5.cloned.1.call-start = ((), (), s32[]{:S(2)}) async-start(), calls=%async_computation | async-start | bytes 226492416 | tf_op jit(solution)/shard_map/psum | solution.py:82
  2034.7 21.7 copy-start
  2089.5 34.7 slice-start.34
  2108.1 16.1 slice-start.35
  2157.3 34.8 slice-start.44
  2176.0 16.1 slice-start.45
  2225.1 62.6 %slice-start.50 = ((s8[4718592]{0:T(1024)(128)(4,1)}), s8[524288]{0:T(1024)(128)(4,1)S(1)}, s32[]{:S(2)}) async-start(s8[4718592]{0:T(1024)(128)(4,1)} %bitcast.331), calls=%async_computation.52 | async-start | bytes 1048576
  2245.3 42.4 %slice-start.51 = ((s8[4718592]{0:T(1024)(128)(4,1)}), s8[4194304]{0:T(1024)(128)(4,1)S(1)}, s32[]{:S(2)}) async-start(s8[4718592]{0:T(1024)(128)(4,1)} %bitcast.331), calls=%async_computation.53 | async-start | bytes 8388608
  2287.7 13.5 copy-start.7
  2287.7 30.5 slice-start.46
  2301.2 17.0 slice-start.47
  2301.2 56.0 %slice-start.48 = ((s8[4718592]{0:T(1024)(128)(4,1)}), s8[4194304]{0:T(1024)(128)(4,1)S(1)}, s32[]{:S(2)}) async-start(s8[4718592]{0:T(1024)(128)(4,1)} %bitcast.329), calls=%async_computation.50 | async-start | bytes 8388608
  2318.2 39.0 slice-start.49
  2357.2 13.5 copy-start.8
  2357.2 30.6 slice-start.40
  2370.7 17.1 slice-start.41
  2370.7 56.6 %slice-start.42 = ((s8[4718592]{0:T(1024)(128)(4,1)}), s8[4194304]{0:T(1024)(128)(4,1)S(1)}, s32[]{:S(2)}) async-start(s8[4718592]{0:T(1024)(128)(4,1)} %bitcast.323), calls=%async_computation.44 | async-start | bytes 8388608
  2387.8 39.5 slice-start.43
  2427.3 13.3 copy-start.9
  2427.3 30.3 slice-start.36
  2440.6 17.0 slice-start.37
  2440.6 56.4 %slice-start.38 = ((s8[4718592]{0:T(1024)(128)(4,1)}), s8[4194304]{0:T(1024)(128)(4,1)S(1)}, s32[]{:S(2)}) async-start(s8[4718592]{0:T(1024)(128)(4,1)} %bitcast.319), calls=%async_computation.40 | async-start | bytes 8388608
  2457.6 39.4 slice-start.39
  2497.1 13.6 copy-start.10
  2497.1 30.7 slice-start.30
  2510.6 17.1 slice-start.31
  2510.6 56.6 %slice-start.32 = ((s8[4718592]{0:T(1024)(128)(4,1)}), s8[4194304]{0:T(1024)(128)(4,1)S(1)}, s32[]{:S(2)}) async-start(s8[4718592]{0:T(1024)(128)(4,1)} %bitcast.313), calls=%async_computation.34 | async-start | bytes 8388608
  2527.8 39.4 slice-start.33
  2567.2 13.6 copy-start.11
  2567.2 13.6 copy-start.17
  2580.9 11.8 copy-start.4
  3889.4 8.8 slice-start.27
  3889.4 8.8 slice-start.28
  3889.4 8.8 slice-start.29
  3898.1 6.9 slice-start.25
  3898.2 7.1 slice-start.26
  3903.6 6.7 slice-start.21
  3910.9 6.6 slice-start.20
  4036.9 8.8 slice-start.12
  4036.9 8.8 slice-start.13
  4036.9 8.8 slice-start.14
  4045.7 6.9 slice-start.10
  4045.7 7.1 slice-start.11
  4051.1 6.7 slice-start.6
  4058.4 6.6 slice-start.5
  (16 other events, 89.4 us)
Sparse Core Ops, SparseCore 0:
  638.2 1248.4 all-reduce.6
  2641.8 1247.5 all-reduce.4
where the time goes:
time: 4150 us; the launch traced here: 4140 us
  waiting for transfers between devices  2420 us (58%)
  matrix products  1180 us (28%)
  other arithmetic  305 us (7%)
  local copies, waits for them, and re-layouts  185 us (4%)
    psum x1, waiting for transfers between devices, local_step(): lax.psum((grads2_in, grads2_out, loss_local), mesh_axes)  1220 us
    psum x1, waiting for transfers between devices, local_step(): grads_in, grads_out = lax.psum((grads_in, grads_out), mesh_axes)  1190 us
    dot_general x12, matrix products, backward(): jnp.einsum('tf,td->fd', post_act, d_hidden, preferred_element_type=jnp.fl...  219 us
    dot_general x10, matrix products, backward(): jnp.einsum('td,fd->tf', d_hidden, out_list[layer_idx], preferred_element_...  217 us
    dot_general x12, matrix products, forward(): jnp.dot(post_act, out_list[layer_idx], preferred_element_type=jnp.float32)  212 us
    dot_general x12, matrix products, backward(): jnp.einsum('td,tf->df', hidden, d_pre, preferred_element_type=jnp.float32)  203 us
    dot_general x12, matrix products, forward(): jnp.dot(hidden, in_list[layer_idx], preferred_element_type=jnp.float32)  198 us
    unnamed x168, local copies, waits for them, and re-layouts  177 us
  transfers between devices with their start and end apart: 2, of which 2 were waited for; matrix products, arithmetic and copies ran while one was open for 1% of the time, Pallas kernels for 0%

commit v1 on v0

v1 whole, which is shorter than its diff:
```python
import jax
import jax.numpy as jnp
import math
from jax import lax
from jax.experimental.layout import Layout, with_layout_constraint
from jax.sharding import PartitionSpec as P

RHO_REL = 0.1
LEARN_RATE = 8.0
SQRT_HALF = 0.7071067811865476
INV_SQRT_2PI = 0.3989422804014327


def gelu_fn(pre_act):
    return 0.5 * pre_act * (1.0 + lax.erf(pre_act * SQRT_HALF))


def gelu_slope(pre_act):
    cdf_part = 0.5 * (1.0 + lax.erf(pre_act * SQRT_HALF))
    return cdf_part + pre_act * INV_SQRT_2PI * jnp.exp(-0.5 * pre_act * pre_act)


def forward(x_rows, in_list, out_list):
    hidden = x_rows
    saved_acts = []
    for layer_idx in range(len(in_list)):
        pre_act = jnp.dot(hidden, in_list[layer_idx], preferred_element_type=jnp.float32).astype(jnp.bfloat16)
        post_act = gelu_fn(pre_act.astype(jnp.float32)).astype(jnp.bfloat16)
        mlp_out = jnp.dot(post_act, out_list[layer_idx], preferred_element_type=jnp.float32)
        saved_acts.append((hidden, pre_act, post_act))
        hidden = (hidden.astype(jnp.float32) + mlp_out).astype(jnp.bfloat16)
    return hidden, saved_acts


def backward(d_top, saved_acts, in_list, out_list, reduce_fn, finish_fn, ahead=3):
    d_hidden = d_top
    n_layers = len(saved_acts)
    pending, finished = [], {}

    def due(value, count):
        while len(pending) > count:
            unit, shard = pending.pop(0)
            finished[unit], value = lax.optimization_barrier((finish_fn(unit, shard), value))
        return value

    for layer_idx in reversed(range(n_layers)):
        hidden, pre_act, post_act = saved_acts[layer_idx]
        d_hidden = due(d_hidden, ahead - 1)
        grad_out = row_major(jnp.einsum('tf,td->fd', post_act, d_hidden, preferred_element_type=jnp.float32))
        grad_out, d_hidden = lax.optimization_barrier((grad_out, d_hidden))
        pending.append((('out', layer_idx), reduce_fn(grad_out)))
        d_hidden = due(d_hidden, ahead - 1)
        d_act = jnp.einsum('td,fd->tf', d_hidden, out_list[layer_idx], preferred_element_type=jnp.float32)
        d_pre = (d_act * gelu_slope(pre_act.astype(jnp.float32))).astype(jnp.bfloat16)
        grad_in = row_major(jnp.einsum('td,tf->df', hidden, d_pre, preferred_element_type=jnp.float32))
        grad_in, d_pre = lax.optimization_barrier((grad_in, d_pre))
        pending.append((('in', layer_idx), reduce_fn(grad_in)))
        if layer_idx > 0:
            back_part = jnp.einsum('tf,df->td', d_pre, in_list[layer_idx], preferred_element_type=jnp.float32)
            d_hidden = (d_hidden.astype(jnp.float32) + back_part).astype(jnp.bfloat16)
    for unit, shard in pending:
        finished[unit] = finish_fn(unit, shard)
    return finished


def row_major(matrix):
    return with_layout_constraint(matrix, Layout(major_to_minor=(0, 1)))


def top_grad(top_hidden, y_rows, inv_count):
    resid_err = top_hidden.astype(jnp.float32) - y_rows.astype(jnp.float32)
    return 0.5 * jnp.sum(resid_err * resid_err), (resid_err * inv_count).astype(jnp.bfloat16)


def solution(mesh):
    mesh_axes = tuple(mesh.axis_names)
    dev_count = math.prod([mesh.shape[axis_name] for axis_name in mesh_axes])
    batch_spec = P(mesh_axes, None, None)

    def local_step(images, targets, w_in, w_out):
        layers, model_dim, hidden_dim = w_in.shape
        tok_local = images.shape[0] * images.shape[1]
        inv_count = 1.0 / (tok_local * dev_count * model_dim)
        radius = RHO_REL * math.sqrt(layers * hidden_dim + model_dim)
        x_rows = images.reshape(tok_local, model_dim)
        y_rows = targets.reshape(tok_local, model_dim)
        my_index = lax.axis_index(mesh_axes)
        rows_in = model_dim // dev_count
        rows_out = hidden_dim // dev_count

        def scatter(grad):
            return row_major(lax.psum_scatter(grad, mesh_axes, scatter_dimension=0, tiled=True))

        def gather(shard):
            return lax.all_gather(shard, mesh_axes, axis=0, tiled=True)

        in_list = [w_in[layer_idx].astype(jnp.bfloat16) for layer_idx in range(layers)]
        out_list = [w_out[layer_idx].astype(jnp.bfloat16) for layer_idx in range(layers)]
        top_hidden, saved_acts = forward(x_rows, in_list, out_list)
        _, d_top = top_grad(top_hidden, y_rows, inv_count)
        w_mine = {}
        for layer_idx in range(layers):
            w_mine['in', layer_idx] = lax.dynamic_slice(w_in, (layer_idx, my_index * rows_in, 0), (1, rows_in, hidden_dim))[0]
            w_mine['out', layer_idx] = lax.dynamic_slice(w_out, (layer_idx, my_index * rows_out, 0), (1, rows_out, model_dim))[0]

        first = backward(d_top, saved_acts, in_list, out_list, scatter, lambda unit, shard: (shard, jnp.sum(shard * shard)))
        norm_sq = lax.psum(sum(part_sq for _, part_sq in first.values()), mesh_axes)
        step_scale = radius / jnp.sqrt(norm_sq)

        def perturbed(unit):
            return gather((w_mine[unit] + step_scale * first[unit][0]).astype(jnp.bfloat16))

        pert_in, pert_out = [], []
        for layer_idx in range(layers):
            pert_in.append(perturbed(('in', layer_idx)))
            pert_out.append(perturbed(('out', layer_idx)))

        top_pert, saved_pert = forward(x_rows, pert_in, pert_out)
        loss_local, d_pert = top_grad(top_pert, y_rows, inv_count)
        second = backward(d_pert, saved_pert, pert_in, pert_out, scatter, lambda unit, shard: shard)
        loss_total = lax.psum(loss_local, mesh_axes)
        full = {unit: gather(shard) for unit, shard in second.items()}
        new_in = [w_in[layer_idx] - LEARN_RATE * full['in', layer_idx] for layer_idx in range(layers)]
        new_out = [w_out[layer_idx] - LEARN_RATE * full['out', layer_idx] for layer_idx in range(layers)]
        return jnp.stack(new_in), jnp.stack(new_out), loss_total * inv_count

    return jax.shard_map(local_step, mesh=mesh, in_specs=(batch_spec, batch_spec, P(), P()), out_specs=(P(), P(), P()), check_vma=False)
```

time: 4150 us -> 3140 us (0.76)
  waiting for transfers between devices: 2420 us -> 1660 us
  local copies, waits for them, and re-layouts: 185 us -> 26.1 us
  other arithmetic: 305 us -> 188 us
    psum x2 -> x0, waiting for transfers between devices: 2420 us -> none  [the longest x1 1220 us: local_step(): lax.psum((grads2_in, grads2_out, loss_local), mesh_axes)]
    reduce_scatter x0 -> x24, waiting for transfers between devices: none -> 932 us  [scatter(): lax.psum_scatter(grad, mesh_axes, scatter_dimension=0, tiled=True)]
    all_gather x0 -> x24, waiting for transfers between devices: none -> 715 us  [gather(): return lax.all_gather(shard, mesh_axes, axis=0, tiled=True)]
    unnamed x168 -> x74, local copies, waits for them, and re-layouts: 177 us -> 26.1 us
    convert_element_type x4 -> x2, other arithmetic: 139 us -> 14.2 us  [perturbed(): (w_mine[unit] + step_scale * first[unit][0]).astype(jnp.bfloat16)]
    unnamed x21 -> x10, other arithmetic: 0.01 us -> 123 us
    sub x2 -> x0, other arithmetic: 110 us -> none  [the longest x1 54.9 us: local_step(): new_in = w_in - LEARN_RATE * jnp.stack(grads2_in)]
    dot_general x10 -> x12, matrix products: 217 us -> 262 us  [backward(): jnp.einsum('td,fd->tf', d_hidden, out_list[layer_idx], preferred_element_...]
  transfers between devices with their start and end apart: 2 -> 48, of which waited for: 2 -> 46; matrix products, arithmetic and copies ran while one was open for 1% -> 33% of each run, Pallas kernels for 0% -> 0%
where the time goes in v1:
time: 3140 us
  waiting for transfers between devices  1660 us (53%)
  matrix products  1190 us (38%)
  other arithmetic  188 us (6%)
  blocking collectives  45 us (1%)
    reduce_scatter x24, waiting for transfers between devices, scatter(): lax.psum_scatter(grad, mesh_axes, scatter_dimension=0, tiled=True)  932 us
    all_gather x24, waiting for transfers between devices, gather(): return lax.all_gather(shard, mesh_axes, axis=0, tiled=True)  715 us
    dot_general x12, matrix products, backward(): jnp.einsum('td,fd->tf', d_hidden, out_list[layer_idx], preferred_element_...  262 us
    dot_general x12, matrix products, forward(): jnp.dot(post_act, out_list[layer_idx], preferred_element_type=jnp.float32)  215 us
    dot_general x12, matrix products, backward(): jnp.einsum('tf,td->fd', post_act, d_hidden, preferred_element_type=jnp.fl...  209 us
    dot_general x12, matrix products, forward(): jnp.dot(hidden, in_list[layer_idx], preferred_element_type=jnp.float32)  202 us
    dot_general x12, matrix products, backward(): jnp.einsum('td,tf->df', hidden, d_pre, preferred_element_type=jnp.float32)  162 us
    dot_general x10, matrix products, backward(): jnp.einsum('tf,df->td', d_pre, in_list[layer_idx], preferred_element_type...  138 us
  transfers between devices with their start and end apart: 48, of which 46 were waited for; matrix products, arithmetic and copies ran while one was open for 33% of the time, Pallas kernels for 0%

profile of v1, /device:TPU:0, one launch (start us, length us, event | category | flops | bytes accessed | tf_op | source)
XLA Modules:
  0.0 3135.3 jit_solution(6091899792838585613)
XLA Ops:
  24.5 18.3 fusion.108
  60.1 18.1 add_convert_fusion.19
  96.1 18.1 add_convert_fusion.18
  131.8 18.1 add_convert_fusion.17
  149.9 18.2 fusion.44
  168.1 18.2 add_convert_fusion.16
  203.7 20.1 fusion.111
  223.9 18.2 fusion.144
  242.1 25.1 fusion.57
  314.9 23.3 fusion.48
  352.1 31.3 reduce-scatter.27.cloned.1.call-done
  418.8 35.5 %reduce-scatter.29.cloned.1.call-done = f32[384,768]{1,0:T(8,128)} async-done(((f32[3072,768]{1,0:T(8,128)}), f32[384,768]{1,0:T(8,128)}) %reduce-scatter.29.cloned.1.call-update) | async-done | bytes 1179664 | tf_op jit(solution)/shard_map/reduce_scatter | solution.py:92
  456.4 23.1 fusion.39
  544.6 51.1 %reduce-scatter.33.cloned.1.call-done = f32[384,768]{1,0:T(8,128)} async-done(((f32[3072,768]{1,0:T(8,128)}), f32[384,768]{1,0:T(8,128)}) %reduce-scatter.33.cloned.1.call-update) | async-done | bytes 1179664 | tf_op jit(solution)/shard_map/reduce_scatter | solution.py:92
  597.9 23.3 fusion.30
  635.1 31.2 reduce-scatter.35.cloned.1.call-done
  701.7 35.5 %reduce-scatter.37.cloned.1.call-done = f32[384,768]{1,0:T(8,128)} async-done(((f32[3072,768]{1,0:T(8,128)}), f32[384,768]{1,0:T(8,128)}) %reduce-scatter.37.cloned.1.call-update) | async-done | bytes 1179664 | tf_op jit(solution)/shard_map/reduce_scatter | solution.py:92
  739.5 23.1 fusion.21
  776.5 31.6 %reduce-scatter.39.cloned.1.call-done = f32[96,3072]{1,0:T(8,128)} async-done(((f32[768,3072]{1,0:T(8,128)}), f32[96,3072]{1,0:T(8,128)}) %reduce-scatter.39.cloned.1.call-update) | async-done | bytes 1179664 | tf_op jit(solution)/shard_map/reduce_scatter | solution.py:92
  843.6 35.3 %reduce-scatter.41.cloned.1.call-done = f32[384,768]{1,0:T(8,128)} async-done(((f32[3072,768]{1,0:T(8,128)}), f32[384,768]{1,0:T(8,128)}) %reduce-scatter.41.cloned.1.call-update) | async-done | bytes 1179664 | tf_op jit(solution)/shard_map/reduce_scatter | solution.py:92
  881.1 23.0 fusion.12
  923.9 25.8 reduce-scatter.43.cloned.1.call-done
  952.7 67.9 %reduce-scatter.45.cloned.1.call-done = f32[384,768]{1,0:T(8,128)} async-done(((f32[3072,768]{1,0:T(8,128)}), f32[384,768]{1,0:T(8,128)}) %reduce-scatter.45.cloned.1.call-update) | async-done | bytes 1179664 | tf_op jit(solution)/shard_map/reduce_scatter | solution.py:92
  1023.4 68.5 %reduce-scatter.47.cloned.1.call-done = f32[96,3072]{1,0:T(8,128)} async-done(((f32[768,3072]{1,0:T(8,128)}), f32[96,3072]{1,0:T(8,128)}) %reduce-scatter.47.cloned.1.call-update) | async-done | bytes 1179664 | tf_op jit(solution)/shard_map/reduce_scatter | solution.py:92
  1094.7 22.2 psum.14
  1138.5 21.6 all-gather.25.cloned.1.call-done
  1175.9 18.8 all-gather.27.cloned.1.call-done
  1211.5 18.4 all-gather.29.cloned.1.call-done
  1245.7 18.8 all-gather.31.cloned.1.call-done
  1315.4 18.4 all-gather.35.cloned.1.call-done
  1384.7 18.5 all-gather.39.cloned.1.call-done
  1454.1 18.6 all-gather.43.cloned.1.call-done
  1523.4 18.8 all-gather.47.cloned.1.call-done
  1542.2 19.8 multiply_reduce_fusion
  1580.1 19.7 fusion.102
  1649.3 19.9 fusion.93
  1699.7 18.7 reduce-scatter.51.cloned.1.call-done
  1735.6 53.5 %reduce-scatter.49.cloned.1.call-done = f32[384,768]{1,0:T(8,128)} async-done(((f32[3072,768]{1,0:T(8,128)}), f32[384,768]{1,0:T(8,128)}) %reduce-scatter.49.cloned.1.call-update) | async-done | bytes 1179664 | tf_op jit(solution)/shard_map/reduce_scatter | solution.py:92
  1789.1 19.9 fusion.84
  1839.6 20.3 reduce-scatter.59.cloned.1.call-done
  1877.2 53.6 %reduce-scatter.57.cloned.1.call-done = f32[384,768]{1,0:T(8,128)} async-done(((f32[3072,768]{1,0:T(8,128)}), f32[384,768]{1,0:T(8,128)}) %reduce-scatter.57.cloned.1.call-update) | async-done | bytes 1179664 | tf_op jit(solution)/shard_map/reduce_scatter | solution.py:92
  1930.8 19.9 fusion.75
  1981.1 20.4 reduce-scatter.55.cloned.1.call-done
  2018.7 53.7 %reduce-scatter.65.cloned.1.call-done = f32[384,768]{1,0:T(8,128)} async-done(((f32[3072,768]{1,0:T(8,128)}), f32[384,768]{1,0:T(8,128)}) %reduce-scatter.65.cloned.1.call-update) | async-done | bytes 1179664 | tf_op jit(solution)/shard_map/reduce_scatter | solution.py:92
  2072.4 20.1 fusion.66
  2122.8 20.5 reduce-scatter.63.cloned.1.call-done
  2160.5 53.5 %reduce-scatter.61.cloned.1.call-done = f32[384,768]{1,0:T(8,128)} async-done(((f32[3072,768]{1,0:T(8,128)}), f32[384,768]{1,0:T(8,128)}) %reduce-scatter.61.cloned.1.call-update) | async-done | bytes 1179664 | tf_op jit(solution)/shard_map/reduce_scatter | solution.py:92
  2214.0 21.6 fusion.4
  2250.8 66.2 %reduce-scatter.67.cloned.1.call-done = f32[96,3072]{1,0:T(8,128)} async-done(((f32[768,3072]{1,0:T(8,128)}), f32[96,3072]{1,0:T(8,128)}) %reduce-scatter.67.cloned.1.call-update) | async-done | bytes 1179664 | tf_op jit(solution)/shard_map/reduce_scatter | solution.py:92
  2317.0 70.8 %reduce-scatter.71.cloned.1.call-done = f32[384,768]{1,0:T(8,128)} async-done(((f32[3072,768]{1,0:T(8,128)}), f32[384,768]{1,0:T(8,128)}) %reduce-scatter.71.cloned.1.call-update) | async-done | bytes 1179664 | tf_op jit(solution)/shard_map/reduce_scatter | solution.py:92
  2387.9 70.7 %reduce-scatter.69.cloned.1.call-done = f32[96,3072]{1,0:T(8,128)} async-done(((f32[768,3072]{1,0:T(8,128)}), f32[96,3072]{1,0:T(8,128)}) %reduce-scatter.69.cloned.1.call-update) | async-done | bytes 1179664 | tf_op jit(solution)/shard_map/reduce_scatter | solution.py:92
  2465.1 22.8 psum.15
  2488.5 25.5 all-gather.49.cloned.1.call-done
  2527.2 41.7 %all-gather.61.cloned.1.call-done = f32[3072,768]{1,0:T(8,128)} async-done(((f32[384,768]{1,0:T(8,128)}), f32[3072,768]{1,0:T(8,128)}) %all-gather.61.cloned.1.call-update) | async-done | bytes 9437200 | tf_op jit(solution)/shard_map/all_gather | solution.py:95
  2580.2 43.3 %all-gather.51.cloned.1.call-done = f32[768,3072]{1,0:T(8,128)} async-done(((f32[96,3072]{1,0:T(8,128)}), f32[768,3072]{1,0:T(8,128)}) %all-gather.51.cloned.1.call-update) | async-done | bytes 9437200 | tf_op jit(solution)/shard_map/all_gather | solution.py:95
  2636.7 41.6 %all-gather.53.cloned.1.call-done = f32[768,3072]{1,0:T(8,128)} async-done(((f32[96,3072]{1,0:T(8,128)}), f32[768,3072]{1,0:T(8,128)}) %all-gather.53.cloned.1.call-update) | async-done | bytes 9437200 | tf_op jit(solution)/shard_map/all_gather | solution.py:95
  2691.5 41.7 %all-gather.55.cloned.1.call-done = f32[768,3072]{1,0:T(8,128)} async-done(((f32[96,3072]{1,0:T(8,128)}), f32[768,3072]{1,0:T(8,128)}) %all-gather.55.cloned.1.call-update) | async-done | bytes 9437200 | tf_op jit(solution)/shard_map/all_gather | solution.py:95
  2746.3 41.7 %all-gather.57.cloned.1.call-done = f32[768,3072]{1,0:T(8,128)} async-done(((f32[96,3072]{1,0:T(8,128)}), f32[768,3072]{1,0:T(8,128)}) %all-gather.57.cloned.1.call-update) | async-done | bytes 9437200 | tf_op jit(solution)/shard_map/all_gather | solution.py:95
  2801.4 41.2 %all-gather.59.cloned.1.call-done = f32[768,3072]{1,0:T(8,128)} async-done(((f32[96,3072]{1,0:T(8,128)}), f32[768,3072]{1,0:T(8,128)}) %all-gather.59.cloned.1.call-update) | async-done | bytes 9437200 | tf_op jit(solution)/shard_map/all_gather | solution.py:95
  2855.7 41.7 %all-gather.63.cloned.1.call-done = f32[3072,768]{1,0:T(8,128)} async-done(((f32[384,768]{1,0:T(8,128)}), f32[3072,768]{1,0:T(8,128)}) %all-gather.63.cloned.1.call-update) | async-done | bytes 9437200 | tf_op jit(solution)/shard_map/all_gather | solution.py:95
  2908.7 43.3 %all-gather.65.cloned.1.call-done = f32[3072,768]{1,0:T(8,128)} async-done(((f32[384,768]{1,0:T(8,128)}), f32[3072,768]{1,0:T(8,128)}) %all-gather.65.cloned.1.call-update) | async-done | bytes 9437200 | tf_op jit(solution)/shard_map/all_gather | solution.py:95
  2963.3 43.3 %all-gather.67.cloned.1.call-done = f32[3072,768]{1,0:T(8,128)} async-done(((f32[384,768]{1,0:T(8,128)}), f32[3072,768]{1,0:T(8,128)}) %all-gather.67.cloned.1.call-update) | async-done | bytes 9437200 | tf_op jit(solution)/shard_map/all_gather | solution.py:95
  3017.9 43.3 %all-gather.69.cloned.1.call-done = f32[3072,768]{1,0:T(8,128)} async-done(((f32[384,768]{1,0:T(8,128)}), f32[3072,768]{1,0:T(8,128)}) %all-gather.69.cloned.1.call-update) | async-done | bytes 9437200 | tf_op jit(solution)/shard_map/all_gather | solution.py:95
  3072.6 43.3 %all-gather.71.cloned.1.call-done = f32[3072,768]{1,0:T(8,128)} async-done(((f32[384,768]{1,0:T(8,128)}), f32[3072,768]{1,0:T(8,128)}) %all-gather.71.cloned.1.call-update) | async-done | bytes 9437200 | tf_op jit(solution)/shard_map/all_gather | solution.py:95
  (252 shorter events, 1075.7 us)
Async XLA Ops:
  7.2 305.6 %reduce-scatter.25.cloned.1.call-start = ((), (), s32[]{:S(2)}) async-start(), calls=%async_computation.24 | async-start | bytes 10616832 | tf_op jit(solution)/shard_map/reduce_scatter | solution.py:92
  242.1 25.2 copy-start.26
  242.1 141.3 %reduce-scatter.27.cloned.1.call-start = ((), (), s32[]{:S(2)}) async-start(), calls=%async_computation.25 | async-start | bytes 10616832 | tf_op jit(solution)/shard_map/reduce_scatter | solution.py:92
  281.0 173.3 %reduce-scatter.29.cloned.1.call-start = ((), (), s32[]{:S(2)}) async-start(), calls=%async_computation.26 | async-start | bytes 10616832 | tf_op jit(solution)/shard_map/reduce_scatter | solution.py:92
  312.7 212.3 %reduce-scatter.31.cloned.1.call-start = ((), (), s32[]{:S(2)}) async-start(), calls=%async_computation.27 | async-start | bytes 10616832 | tf_op jit(solution)/shard_map/reduce_scatter | solution.py:92
  352.0 243.7 %reduce-scatter.33.cloned.1.call-start = ((), (), s32[]{:S(2)}) async-start(), calls=%async_computation.28 | async-start | bytes 10616832 | tf_op jit(solution)/shard_map/reduce_scatter | solution.py:92
  418.7 37.7 %copy-start.34 = (bf16[1728,768]{1,0:T(8,128)(2,1)S(1)}, bf16[1728,768]{1,0:T(8,128)(2,1)}, u32[]{:S(2)}) copy-start(bf16[1728,768]{1,0:T(8,128)(2,1)} %copy-done.33) | copy-start | bytes 7962628
  418.7 247.7 %reduce-scatter.35.cloned.1.call-start = ((), (), s32[]{:S(2)}) async-start(), calls=%async_computation.29 | async-start | bytes 10616832 | tf_op jit(solution)/shard_map/reduce_scatter | solution.py:92
  493.4 243.8 %reduce-scatter.37.cloned.1.call-start = ((), (), s32[]{:S(2)}) async-start(), calls=%async_computation.30 | async-start | bytes 10616832 | tf_op jit(solution)/shard_map/reduce_scatter | solution.py:92
  544.5 263.6 %reduce-scatter.39.cloned.1.call-start = ((), (), s32[]{:S(2)}) async-start(), calls=%async_computation.31 | async-start | bytes 10616832 | tf_op jit(solution)/shard_map/reduce_scatter | solution.py:92
  635.1 243.8 %reduce-scatter.41.cloned.1.call-start = ((), (), s32[]{:S(2)}) async-start(), calls=%async_computation.32 | async-start | bytes 10616832 | tf_op jit(solution)/shard_map/reduce_scatter | solution.py:92
  701.7 37.8 %copy-start.30 = (bf16[1728,768]{1,0:T(8,128)(2,1)S(1)}, bf16[1728,768]{1,0:T(8,128)(2,1)}, u32[]{:S(2)}) copy-start(bf16[1728,768]{1,0:T(8,128)(2,1)} %copy-done.29) | copy-start | bytes 7962628
  701.7 248.0 %reduce-scatter.43.cloned.1.call-start = ((), (), s32[]{:S(2)}) async-start(), calls=%async_computation.33 | async-start | bytes 10616832 | tf_op jit(solution)/shard_map/reduce_scatter | solution.py:92
  776.4 244.1 %reduce-scatter.45.cloned.1.call-start = ((), (), s32[]{:S(2)}) async-start(), calls=%async_computation.34 | async-start | bytes 10616832 | tf_op jit(solution)/shard_map/reduce_scatter | solution.py:92
  843.5 37.6 %copy-start.36 = (bf16[1728,768]{1,0:T(8,128)(2,1)S(1)}, bf16[1728,768]{1,0:T(8,128)(2,1)}, u32[]{:S(2)}) copy-start(bf16[1728,768]{1,0:T(8,128)(2,1)} %copy-done.35) | copy-start | bytes 7962628
  843.6 248.3 %reduce-scatter.47.cloned.1.call-start = ((), (), s32[]{:S(2)}) async-start(), calls=%async_computation.35 | async-start | bytes 10616832 | tf_op jit(solution)/shard_map/reduce_scatter | solution.py:92
  918.0 199.6 %copy-start.2 = (f32[96,3072]{1,0:T(8,128)S(1)}, f32[96,3072]{1,0:T(8,128)}, u32[]{:S(2)}) copy-start(f32[96,3072]{1,0:T(8,128)} %reduce-scatter.27.cloned.1.call-done) | copy-start | bytes 3538948
  918.0 242.0 %all-gather.25.cloned.1.call-start = ((), (), s32[]{:S(2)}) async-start(), calls=%async_computation.36 | async-start | bytes 5308416 | tf_op jit(solution)/shard_map/all_gather | solution.py:95
  951.9 173.2 %copy-start = (f32[384,768]{1,0:T(8,128)S(1)}, f32[384,768]{1,0:T(8,128)}, u32[]{:S(2)}) copy-start(f32[384,768]{1,0:T(8,128)} %reduce-scatter.25.cloned.1.call-done) | copy-start | bytes 3538948
  951.9 173.2 %copy-start.1 = (f32[384,768]{1,0:T(8,128)S(1)}, f32[384,768]{1,0:T(8,128)}, u32[]{:S(2)}) copy-start(f32[384,768]{1,0:T(8,128)} %reduce-scatter.29.cloned.1.call-done) | copy-start | bytes 3538948
  1125.0 69.6 %all-gather.27.cloned.1.call-start = ((), (), s32[]{:S(2)}) async-start(), calls=%async_computation.37 | async-start | bytes 5308416 | tf_op jit(solution)/shard_map/all_gather | solution.py:95
  1131.9 98.0 %all-gather.29.cloned.1.call-start = ((), (), s32[]{:S(2)}) async-start(), calls=%async_computation.38 | async-start | bytes 5308416 | tf_op jit(solution)/shard_map/all_gather | solution.py:95
  1132.5 132.0 %all-gather.31.cloned.1.call-start = ((), (), s32[]{:S(2)}) async-start(), calls=%async_computation.39 | async-start | bytes 5308416 | tf_op jit(solution)/shard_map/all_gather | solution.py:95
  1133.1 166.1 %all-gather.33.cloned.1.call-start = ((), (), s32[]{:S(2)}) async-start(), calls=%async_computation.40 | async-start | bytes 5308416 | tf_op jit(solution)/shard_map/all_gather | solution.py:95
  1133.7 200.1 %all-gather.35.cloned.1.call-start = ((), (), s32[]{:S(2)}) async-start(), calls=%async_computation.41 | async-start | bytes 5308416 | tf_op jit(solution)/shard_map/all_gather | solution.py:95
  1134.3 234.3 %all-gather.37.cloned.1.call-start = ((), (), s32[]{:S(2)}) async-start(), calls=%async_computation.42 | async-start | bytes 5308416 | tf_op jit(solution)/shard_map/all_gather | solution.py:95
  1135.0 268.2 %all-gather.39.cloned.1.call-start = ((), (), s32[]{:S(2)}) async-start(), calls=%async_computation.43 | async-start | bytes 5308416 | tf_op jit(solution)/shard_map/all_gather | solution.py:95
  1135.6 302.4 %all-gather.41.cloned.1.call-start = ((), (), s32[]{:S(2)}) async-start(), calls=%async_computation.44 | async-start | bytes 5308416 | tf_op jit(solution)/shard_map/all_gather | solution.py:95
  1136.3 336.4 %all-gather.43.cloned.1.call-start = ((), (), s32[]{:S(2)}) async-start(), calls=%async_computation.45 | async-start | bytes 5308416 | tf_op jit(solution)/shard_map/all_gather | solution.py:95
  1137.1 370.5 %all-gather.45.cloned.1.call-start = ((), (), s32[]{:S(2)}) async-start(), calls=%async_computation.46 | async-start | bytes 5308416 | tf_op jit(solution)/shard_map/all_gather | solution.py:95
  1137.8 404.4 %all-gather.47.cloned.1.call-start = ((), (), s32[]{:S(2)}) async-start(), calls=%async_computation.47 | async-start | bytes 5308416 | tf_op jit(solution)/shard_map/all_gather | solution.py:95
  1138.4 56.3 %copy-start.7 = (bf16[3,576,768]{2,1,0:T(8,128)(2,1)S(1)}, bf16[3,576,768]{2,1,0:T(8,128)(2,1)}, u32[]{:S(2)}) copy-start(bf16[3,576,768]{2,1,0:T(8,128)(2,1)} %param.4) | copy-start | bytes 7962628
  1138.4 510.9 %reduce-scatter.53.cloned.1.call-start = ((), (), s32[]{:S(2)}) async-start(), calls=%async_computation.50 | async-start | bytes 10616832 | tf_op jit(solution)/shard_map/reduce_scatter | solution.py:92
  1211.5 53.0 %copy-start.14 = (bf16[1728,768]{1,0:T(8,128)(2,1)S(1)}, bf16[1728,768]{1,0:T(8,128)(2,1)}, u32[]{:S(2)}) copy-start(bf16[1728,768]{1,0:T(8,128)(2,1)} %fusion.109) | copy-start | bytes 7962628
  1281.4 52.4 %copy-start.15 = (bf16[1728,768]{1,0:T(8,128)(2,1)S(1)}, bf16[1728,768]{1,0:T(8,128)(2,1)}, u32[]{:S(2)}) copy-start(bf16[1728,768]{1,0:T(8,128)(2,1)} %add_convert_fusion.9) | copy-start | bytes 7962628
  1350.7 52.5 %copy-start.20 = (bf16[1728,768]{1,0:T(8,128)(2,1)S(1)}, bf16[1728,768]{1,0:T(8,128)(2,1)}, u32[]{:S(2)}) copy-start(bf16[1728,768]{1,0:T(8,128)(2,1)} %add_convert_fusion.8) | copy-start | bytes 7962628
  1419.9 52.8 %copy-start.23 = (bf16[1728,768]{1,0:T(8,128)(2,1)S(1)}, bf16[1728,768]{1,0:T(8,128)(2,1)}, u32[]{:S(2)}) copy-start(bf16[1728,768]{1,0:T(8,128)(2,1)} %add_convert_fusion.7) | copy-start | bytes 7962628
  1489.6 52.6 %copy-start.4 = (bf16[3,576,768]{2,1,0:T(8,128)(2,1)S(1)}, bf16[3,576,768]{2,1,0:T(8,128)(2,1)}, u32[]{:S(2)}) copy-start(bf16[3,576,768]{2,1,0:T(8,128)(2,1)} %param.5) | copy-start | bytes 7962628
  1580.1 138.3 %reduce-scatter.51.cloned.1.call-start = ((), (), s32[]{:S(2)}) async-start(), calls=%async_computation.49 | async-start | bytes 10616832 | tf_op jit(solution)/shard_map/reduce_scatter | solution.py:92
  1616.9 172.2 %reduce-scatter.49.cloned.1.call-start = ((), (), s32[]{:S(2)}) async-start(), calls=%async_computation.48 | async-start | bytes 10616832 | tf_op jit(solution)/shard_map/reduce_scatter | solution.py:92
  1649.3 210.6 %reduce-scatter.59.cloned.1.call-start = ((), (), s32[]{:S(2)}) async-start(), calls=%async_computation.53 | async-start | bytes 10616832 | tf_op jit(solution)/shard_map/reduce_scatter | solution.py:92
  1686.4 244.4 %reduce-scatter.57.cloned.1.call-start = ((), (), s32[]{:S(2)}) async-start(), calls=%async_computation.52 | async-start | bytes 10616832 | tf_op jit(solution)/shard_map/reduce_scatter | solution.py:92
  1699.7 35.9 %copy-start.27 = (bf16[1728,768]{1,0:T(8,128)(2,1)}, bf16[1728,768]{1,0:T(8,128)(2,1)S(1)}, u32[]{:S(2)}) copy-start(bf16[1728,768]{1,0:T(8,128)(2,1)S(1)} %add_convert_fusion.3) | copy-start | bytes 7962628
  1735.5 266.0 %reduce-scatter.55.cloned.1.call-start = ((), (), s32[]{:S(2)}) async-start(), calls=%async_computation.51 | async-start | bytes 10616832 | tf_op jit(solution)/shard_map/reduce_scatter | solution.py:92
  1826.1 246.2 %reduce-scatter.65.cloned.1.call-start = ((), (), s32[]{:S(2)}) async-start(), calls=%async_computation.56 | async-start | bytes 10616832 | tf_op jit(solution)/shard_map/reduce_scatter | solution.py:92
  1839.6 37.5 %copy-start.28 = (bf16[1728,768]{1,0:T(8,128)(2,1)}, bf16[1728,768]{1,0:T(8,128)(2,1)S(1)}, u32[]{:S(2)}) copy-start(bf16[1728,768]{1,0:T(8,128)(2,1)S(1)} %add_convert_fusion.2) | copy-start | bytes 7962628
  1877.1 266.2 %reduce-scatter.63.cloned.1.call-start = ((), (), s32[]{:S(2)}) async-start(), calls=%async_computation.55 | async-start | bytes 10616832 | tf_op jit(solution)/shard_map/reduce_scatter | solution.py:92
  1967.9 246.1 %reduce-scatter.61.cloned.1.call-start = ((), (), s32[]{:S(2)}) async-start(), calls=%async_computation.54 | async-start | bytes 10616832 | tf_op jit(solution)/shard_map/reduce_scatter | solution.py:92
  1981.1 37.5 %copy-start.32 = (bf16[1728,768]{1,0:T(8,128)(2,1)}, bf16[1728,768]{1,0:T(8,128)(2,1)S(1)}, u32[]{:S(2)}) copy-start(bf16[1728,768]{1,0:T(8,128)(2,1)S(1)} %add_convert_fusion.1) | copy-start | bytes 7962628
  2018.6 298.3 %reduce-scatter.67.cloned.1.call-start = ((), (), s32[]{:S(2)}) async-start(), calls=%async_computation.57 | async-start | bytes 10616832 | tf_op jit(solution)/shard_map/reduce_scatter | solution.py:92
  2249.4 138.4 %reduce-scatter.71.cloned.1.call-start = ((), (), s32[]{:S(2)}) async-start(), calls=%async_computation.65 | async-start | bytes 10616832 | tf_op jit(solution)/shard_map/reduce_scatter | solution.py:92
  2250.1 208.4 %reduce-scatter.69.cloned.1.call-start = ((), (), s32[]{:S(2)}) async-start(), calls=%async_computation.59 | async-start | bytes 10616832 | tf_op jit(solution)/shard_map/reduce_scatter | solution.py:92
  2250.7 263.3 %all-gather.49.cloned.1.call-start = ((), (), s32[]{:S(2)}) async-start(), calls=%async_computation.58 | async-start | bytes 10616832 | tf_op jit(solution)/shard_map/all_gather | solution.py:95
  2316.9 252.0 %all-gather.61.cloned.1.call-start = ((), (), s32[]{:S(2)}) async-start(), calls=%async_computation.66 | async-start | bytes 10616832 | tf_op jit(solution)/shard_map/all_gather | solution.py:95
  2387.8 235.7 %all-gather.51.cloned.1.call-start = ((), (), s32[]{:S(2)}) async-start(), calls=%async_computation.60 | async-start | bytes 10616832 | tf_op jit(solution)/shard_map/all_gather | solution.py:95
  2458.5 219.8 %all-gather.53.cloned.1.call-start = ((), (), s32[]{:S(2)}) async-start(), calls=%async_computation.61 | async-start | bytes 10616832 | tf_op jit(solution)/shard_map/all_gather | solution.py:95
  2459.3 273.9 %all-gather.55.cloned.1.call-start = ((), (), s32[]{:S(2)}) async-start(), calls=%async_computation.62 | async-start | bytes 10616832 | tf_op jit(solution)/shard_map/all_gather | solution.py:95
  2460.0 327.9 %all-gather.57.cloned.1.call-start = ((), (), s32[]{:S(2)}) async-start(), calls=%async_computation.63 | async-start | bytes 10616832 | tf_op jit(solution)/shard_map/all_gather | solution.py:95
  2460.8 381.8 %all-gather.59.cloned.1.call-start = ((), (), s32[]{:S(2)}) async-start(), calls=%async_computation.64 | async-start | bytes 10616832 | tf_op jit(solution)/shard_map/all_gather | solution.py:95
  2461.3 436.0 %all-gather.63.cloned.1.call-start = ((), (), s32[]{:S(2)}) async-start(), calls=%async_computation.67 | async-start | bytes 10616832 | tf_op jit(solution)/shard_map/all_gather | solution.py:95
  2462.1 489.9 %all-gather.65.cloned.1.call-start = ((), (), s32[]{:S(2)}) async-start(), calls=%async_computation.68 | async-start | bytes 10616832 | tf_op jit(solution)/shard_map/all_gather | solution.py:95
  2462.7 543.9 %all-gather.67.cloned.1.call-start = ((), (), s32[]{:S(2)}) async-start(), calls=%async_computation.69 | async-start | bytes 10616832 | tf_op jit(solution)/shard_map/all_gather | solution.py:95
  2463.3 598.0 %all-gather.69.cloned.1.call-start = ((), (), s32[]{:S(2)}) async-start(), calls=%async_computation.70 | async-start | bytes 10616832 | tf_op jit(solution)/shard_map/all_gather | solution.py:95
  2463.8 652.1 %all-gather.71.cloned.1.call-start = ((), (), s32[]{:S(2)}) async-start(), calls=%async_computation.71 | async-start | bytes 10616832 | tf_op jit(solution)/shard_map/all_gather | solution.py:95
  (21 other events, 269.1 us)
Sparse Core Ops, SparseCore 0:
  242.2 70.2 reduce-scatter.24
  315.9 67.4 reduce-scatter.26
  386.8 67.4 reduce-scatter.28
  457.5 67.4 reduce-scatter.30
  528.2 67.3 reduce-scatter.32
  599.0 67.3 reduce-scatter.34
  669.8 67.3 reduce-scatter.36
  740.6 67.3 reduce-scatter.38
  811.5 67.3 reduce-scatter.40
  882.2 67.4 reduce-scatter.42
  953.1 67.3 reduce-scatter.44
  1024.4 67.4 reduce-scatter.46
  1125.2 34.8 all-gather.24
  1161.7 32.9 all-gather.26
  1196.9 32.9 all-gather.28
  1231.6 32.9 all-gather.30
  1266.2 32.9 all-gather.32
  1300.8 32.9 all-gather.34
  1335.6 32.9 all-gather.36
  1370.2 32.9 all-gather.38
  1405.0 32.9 all-gather.40
  1439.8 32.9 all-gather.42
  1474.6 32.9 all-gather.44
  1509.2 32.9 all-gather.46
  1580.2 67.4 reduce-scatter.52
  1650.9 67.4 reduce-scatter.50
  1721.6 67.3 reduce-scatter.48
  1792.5 67.3 reduce-scatter.58
  1863.3 67.4 reduce-scatter.56
  1934.1 67.4 reduce-scatter.54
  2005.0 67.3 reduce-scatter.64
  2075.8 67.4 reduce-scatter.62
  2146.5 67.4 reduce-scatter.60
  2249.5 67.3 reduce-scatter.66
  2320.3 67.4 reduce-scatter.70
  2391.1 67.4 reduce-scatter.68
  2460.2 53.7 all-gather.48
  2515.8 53.0 all-gather.60
  2570.6 52.9 all-gather.50
  2625.4 52.9 all-gather.52
  2680.2 52.9 all-gather.54
  2734.9 52.9 all-gather.56
  2789.6 52.9 all-gather.58
  2844.4 52.9 all-gather.62
  2899.0 52.9 all-gather.64
  2953.6 52.9 all-gather.66
  3008.3 52.9 all-gather.68
  3062.9 52.9 all-gather.70

commit v2 on v1

--- a/solution.py
+++ b/solution.py
@@ -32,35 +32,61 @@
     return hidden, saved_acts
 
 
-def backward(d_top, saved_acts, in_list, out_list, reduce_fn, finish_fn, ahead=3):
+def backward(d_top, saved_acts, in_list, out_list, reduce_fn, finish_fn, groups):
     d_hidden = d_top
     n_layers = len(saved_acts)
-    pending, finished = [], {}
+    made, waiting, finished = {}, [], {}
 
-    def due(value, count):
-        while len(pending) > count:
-            unit, shard = pending.pop(0)
-            finished[unit], value = lax.optimization_barrier((finish_fn(unit, shard), value))
+    def due(value, unit_idx):
+        while waiting and waiting[0][0] <= unit_idx:
+            _, kind, members, shard = waiting.pop(0)
+            shard, value = lax.optimization_barrier((finish_fn(kind, members, shard), value))
+            finished[kind, members] = shard
         return value
 
+    def launch(kind, layer_idx, grad):
+        made[kind, layer_idx] = grad
+        for group_kind, members, due_unit in groups:
+            if group_kind == kind and min(members) == layer_idx:
+                parts = [made[kind, member] for member in members]
+                joined = parts[0] if len(parts) == 1 else row_major(jnp.concatenate(parts, axis=1))
+                waiting.append((due_unit, kind, members, reduce_fn(joined)))
+
     for layer_idx in reversed(range(n_layers)):
+        unit_idx = 2 * (n_layers - 1 - layer_idx)
         hidden, pre_act, post_act = saved_acts[layer_idx]
-        d_hidden = due(d_hidden, ahead - 1)
+        d_hidden = due(d_hidden, unit_idx)
         grad_out = row_major(jnp.einsum('tf,td->fd', post_act, d_hidden, preferred_element_type=jnp.float32))
         grad_out, d_hidden = lax.optimization_barrier((grad_out, d_hidden))
-        pending.append((('out', layer_idx), reduce_fn(grad_out)))
-        d_hidden = due(d_hidden, ahead - 1)
+        launch('out', layer_idx, grad_out)
+        d_hidden = due(d_hidden, unit_idx + 1)
         d_act = jnp.einsum('td,fd->tf', d_hidden, out_list[layer_idx], preferred_element_type=jnp.float32)
         d_pre = (d_act * gelu_slope(pre_act.astype(jnp.float32))).astype(jnp.bfloat16)
         grad_in = row_major(jnp.einsum('td,tf->df', hidden, d_pre, preferred_element_type=jnp.float32))
         grad_in, d_pre = lax.optimization_barrier((grad_in, d_pre))
-        pending.append((('in', layer_idx), reduce_fn(grad_in)))
+        launch('in', layer_idx, grad_in)
         if layer_idx > 0:
             back_part = jnp.einsum('tf,df->td', d_pre, in_list[layer_idx], preferred_element_type=jnp.float32)
             d_hidden = (d_hidden.astype(jnp.float32) + back_part).astype(jnp.bfloat16)
-    for unit, shard in pending:
-        finished[unit] = finish_fn(unit, shard)
+    for _, kind, members, shard in waiting:
+        finished[kind, members] = finish_fn(kind, members, shard)
     return finished
+
+
+def reduce_groups(n_layers):
+    last, groups = 2 * n_layers, []
+    for top, size, due_out in ((n_layers - 1, 1, 4), (n_layers - 2, 2, 8), (n_layers - 4, n_layers - 3, last)):
+        members = tuple(range(top, top - size, -1))
+        groups += [('out', members, due_out), ('in', members, due_out + (3 if size == 2 else 1))]
+    return groups
+
+
+def per_layer(groups_done, width):
+    split = {}
+    for (kind, members), shard in groups_done.items():
+        for pos, layer_idx in enumerate(members):
+            split[kind, layer_idx] = lax.slice_in_dim(shard, pos * width[kind], (pos + 1) * width[kind], axis=1)
+    return split
 
 
 def row_major(matrix):
@@ -98,28 +124,38 @@
         out_list = [w_out[layer_idx].astype(jnp.bfloat16) for layer_idx in range(layers)]
         top_hidden, saved_acts = forward(x_rows, in_list, out_list)
         _, d_top = top_grad(top_hidden, y_rows, inv_count)
-        w_mine = {}
-        for layer_idx in range(layers):
-            w_mine['in', layer_idx] = lax.dynamic_slice(w_in, (layer_idx, my_index * rows_in, 0), (1, rows_in, hidden_dim))[0]
-            w_mine['out', layer_idx] = lax.dynamic_slice(w_out, (layer_idx, my_index * rows_out, 0), (1, rows_out, model_dim))[0]
+        width = {'in': hidden_dim, 'out': model_dim}
+        groups = reduce_groups(layers)
 
-        first = backward(d_top, saved_acts, in_list, out_list, scatter, lambda unit, shard: (shard, jnp.sum(shard * shard)))
+        def mine(kind, layer_idx):
+            if kind == 'in':
+                return lax.dynamic_slice(w_in, (layer_idx, my_index * rows_in, 0), (1, rows_in, hidden_dim))[0]
+            return lax.dynamic_slice(w_out, (layer_idx, my_index * rows_out, 0), (1, rows_out, model_dim))[0]
+
+        def gather_layers(kind, members, shards):
+            joined = shards[0] if len(shards) == 1 else row_major(jnp.concatenate(shards, axis=1))
+            return per_layer({(kind, members): gather(joined)}, width)
+
+        first = backward(d_top, saved_acts, in_list, out_list, scatter, lambda kind, members, shard: (shard, jnp.sum(shard * shard)), groups)
         norm_sq = lax.psum(sum(part_sq for _, part_sq in first.values()), mesh_axes)
         step_scale = radius / jnp.sqrt(norm_sq)
-
-        def perturbed(unit):
-            return gather((w_mine[unit] + step_scale * first[unit][0]).astype(jnp.bfloat16))
-
-        pert_in, pert_out = [], []
-        for layer_idx in range(layers):
-            pert_in.append(perturbed(('in', layer_idx)))
-            pert_out.append(perturbed(('out', layer_idx)))
+        first = per_layer({group: shard for group, (shard, _) in first.items()}, width)
+        pert = {}
+        for members in ((0,), (1, 2), (3, 4), (5,)):
+            for kind in ('in', 'out'):
+                shards = [(mine(kind, layer_idx) + step_scale * first[kind, layer_idx]).astype(jnp.bfloat16) for layer_idx in members]
+                pert.update(gather_layers(kind, members, shards))
+        pert_in = [pert['in', layer_idx] for layer_idx in range(layers)]
+        pert_out = [pert['out', layer_idx] for layer_idx in range(layers)]
 
         top_pert, saved_pert = forward(x_rows, pert_in, pert_out)
         loss_local, d_pert = top_grad(top_pert, y_rows, inv_count)
-        second = backward(d_pert, saved_pert, pert_in, pert_out, scatter, lambda unit, shard: shard)
+        second = per_layer(backward(d_pert, saved_pert, pert_in, pert_out, scatter, lambda kind, members, shard: shard, groups), width)
         loss_total = lax.psum(loss_local, mesh_axes)
-        full = {unit: gather(shard) for unit, shard in second.items()}
+        full = {}
+        for members in ((5, 4, 3), (2, 1, 0)):
+            for kind in ('out', 'in'):
+                full.update(gather_layers(kind, members, [second[kind, layer_idx] for layer_idx in members]))
         new_in = [w_in[layer_idx] - LEARN_RATE * full['in', layer_idx] for layer_idx in range(layers)]
         new_out = [w_out[layer_idx] - LEARN_RATE * full['out', layer_idx] for layer_idx in range(layers)]
         return jnp.stack(new_in), jnp.stack(new_out), loss_total * inv_count

time: 3140 us -> 2720 us (0.87)
  waiting for transfers between devices: 1660 us -> 1100 us
  other arithmetic: 188 us -> 329 us
    reduce_scatter x24 -> x12, waiting for transfers between devices: 932 us -> 532 us  [scatter(): lax.psum_scatter(grad, mesh_axes, scatter_dimension=0, tiled=True)]
    concatenate x0 -> x14, other arithmetic: none -> 149 us  [the longest x8 135 us: launch(): jnp.concatenate(parts, axis=1)]
    all_gather x24 -> x12, waiting for transfers between devices: 715 us -> 568 us  [gather(): return lax.all_gather(shard, mesh_axes, axis=0, tiled=True)]
    unnamed x10 -> x13, other arithmetic: 123 us -> 123 us
  transfers between devices with their start and end apart: 48 -> 24, of which waited for: 46 -> 16; matrix products, arithmetic and copies ran while one was open for 33% -> 44% of each run, Pallas kernels for 0% -> 0%
where the time goes in v2:
time: 2720 us; the launch traced here: 2710 us
  matrix products  1200 us (44%)
  waiting for transfers between devices  1100 us (40%)
  other arithmetic  329 us (12%)
  blocking collectives  45.2 us (2%)
    all_gather x12, waiting for transfers between devices, gather(): return lax.all_gather(shard, mesh_axes, axis=0, tiled=True)  568 us
    reduce_scatter x12, waiting for transfers between devices, scatter(): lax.psum_scatter(grad, mesh_axes, scatter_dimension=0, tiled=True)  532 us
    dot_general x12, matrix products, backward(): jnp.einsum('td,fd->tf', d_hidden, out_list[layer_idx], preferred_element_...  279 us
    dot_general x12, matrix products, forward(): jnp.dot(post_act, out_list[layer_idx], preferred_element_type=jnp.float32)  215 us
    dot_general x12, matrix products, backward(): jnp.einsum('tf,td->fd', post_act, d_hidden, preferred_element_type=jnp.fl...  213 us
    dot_general x12, matrix products, forward(): jnp.dot(hidden, in_list[layer_idx], preferred_element_type=jnp.float32)  202 us
    dot_general x12, matrix products, backward(): jnp.einsum('td,tf->df', hidden, d_pre, preferred_element_type=jnp.float32)  165 us
    concatenate x8, other arithmetic, launch(): jnp.concatenate(parts, axis=1)  135 us
  transfers between devices with their start and end apart: 24, of which 16 were waited for; matrix products, arithmetic and copies ran while one was open for 44% of the time, Pallas kernels for 0%

profile of v2, /device:TPU:0, one launch (start us, length us, event | category | flops | bytes accessed | tf_op | source)
XLA Modules:
  0.0 2708.2 jit_solution(3406294489507033713)
XLA Ops:
  7.2 17.3 fusion.8
  24.5 18.2 fusion.144
  42.8 17.3 fusion.17
  60.1 18.1 add_convert_fusion.19
  78.2 17.9 fusion.26
  96.1 18.1 add_convert_fusion.18
  114.2 17.3 fusion.35
  131.5 18.1 add_convert_fusion.17
  149.6 18.2 fusion.44
  167.8 18.2 add_convert_fusion.16
  186.0 17.4 fusion.53
  203.4 20.2 fusion.147
  223.5 18.1 fusion.226
  241.8 25.2 fusion.57
  295.4 18.3 fusion.229
  313.7 22.8 fusion.48
  364.7 17.2 fusion.232
  399.5 22.9 fusion.39
  460.5 17.5 fusion.235
  478.0 25.3 fusion.30
  533.1 17.3 fusion.238
  550.4 22.9 fusion.21
  599.6 17.2 fusion.241
  616.8 20.9 pad_maximum_fusion
  640.9 22.9 fusion.12
  677.6 21.1 pad_maximum_fusion.1
  701.3 101.2 %reduce-scatter.21.cloned.1.call-done = f32[384,2304]{1,0:T(8,128)} async-done(((f32[3072,2304]{1,0:T(8,128)}), f32[384,2304]{1,0:T(8,128)}) %reduce-scatter.21.cloned.1.call-update) | async-done | bytes 3538960 | tf_op jit(solution)/shard_map/reduce_scatter | solution.py:118
  806.7 160.8 %reduce-scatter.23.cloned.1.call-done = f32[96,9216]{1,0:T(8,128)} async-done(((f32[768,9216]{1,0:T(8,128)}), f32[96,9216]{1,0:T(8,128)}) %reduce-scatter.23.cloned.1.call-update) | async-done | bytes 3538960 | tf_op jit(solution)/shard_map/reduce_scatter | solution.py:118
  971.7 22.2 psum.14
  1019.2 18.3 all-gather.13.cloned.1.call-done
  1053.3 18.9 all-gather.15.cloned.1.call-done
  1072.2 16.8 fusion.145
  1089.1 38.5 %all-gather.17.cloned.1.call-done = bf16[768,6144]{1,0:T(8,128)(2,1)} async-done(((bf16[96,6144]{1,0:T(8,128)(2,1)}), bf16[768,6144]{1,0:T(8,128)(2,1)}) %all-gather.17.cloned.1.call-update) | async-done | bytes 9437200 | tf_op jit(solution)/shard_map/all_gather | solution.py:121
  1143.5 38.8 %all-gather.19.cloned.1.call-done = bf16[3072,1536]{1,0:T(8,128)(2,1)} async-done(((bf16[384,1536]{1,0:T(8,128)(2,1)}), bf16[3072,1536]{1,0:T(8,128)(2,1)}) %all-gather.19.cloned.1.call-update) | async-done | bytes 9437200 | tf_op jit(solution)/shard_map/all_gather | solution.py:121
  1182.2 16.8 add_convert_fusion.9
  1199.0 16.6 fusion.71
  1215.6 16.8 add_convert_fusion.8
  1252.9 38.8 %all-gather.23.cloned.1.call-done = bf16[3072,1536]{1,0:T(8,128)(2,1)} async-done(((bf16[384,1536]{1,0:T(8,128)(2,1)}), bf16[3072,1536]{1,0:T(8,128)(2,1)}) %all-gather.23.cloned.1.call-update) | async-done | bytes 9437200 | tf_op jit(solution)/shard_map/all_gather | solution.py:121
  1291.7 16.8 add_convert_fusion.7
  1308.5 16.3 fusion.89
  1324.8 16.9 add_convert_fusion.6
  1341.6 16.1 fusion.98
  1361.1 19.8 multiply_reduce_fusion
  1380.9 18.1 fusion.211
  1399.0 19.9 fusion.102
  1451.0 17.5 fusion.214
  1468.5 24.1 fusion.93
  1518.6 18.0 fusion.217
  1551.7 20.6 fusion.84
  1611.9 17.6 fusion.220
  1629.5 24.0 fusion.75
  1679.5 17.9 fusion.223
  1697.5 24.7 fusion.66
  1747.9 18.1 fusion.208
  1766.0 20.9 pad_maximum_fusion.3
  1789.3 24.0 fusion.4
  1827.1 21.1 pad_maximum_fusion.2
  1848.2 106.3 %reduce-scatter.35.cloned.1.call-done = f32[384,2304]{1,0:T(8,128)} async-done(((f32[3072,2304]{1,0:T(8,128)}), f32[384,2304]{1,0:T(8,128)}) %reduce-scatter.35.cloned.1.call-update) | async-done | bytes 3538960 | tf_op jit(solution)/shard_map/reduce_scatter | solution.py:118
  1958.7 160.9 %reduce-scatter.33.cloned.1.call-done = f32[96,9216]{1,0:T(8,128)} async-done(((f32[768,9216]{1,0:T(8,128)}), f32[96,9216]{1,0:T(8,128)}) %reduce-scatter.33.cloned.1.call-update) | async-done | bytes 3538960 | tf_op jit(solution)/shard_map/reduce_scatter | solution.py:118
  2122.3 23.0 psum.15
  2145.9 109.3 %all-gather.33.cloned.1.call-done = f32[3072,2304]{1,0:T(8,128)} async-done(((f32[384,2304]{1,0:T(8,128)}), f32[3072,2304]{1,0:T(8,128)}) %all-gather.33.cloned.1.call-update) | async-done | bytes 28311568 | tf_op jit(solution)/shard_map/all_gather | solution.py:121
  2289.2 101.4 %all-gather.35.cloned.1.call-done = f32[3072,2304]{1,0:T(8,128)} async-done(((f32[384,2304]{1,0:T(8,128)}), f32[3072,2304]{1,0:T(8,128)}) %all-gather.35.cloned.1.call-update) | async-done | bytes 28311568 | tf_op jit(solution)/shard_map/all_gather | solution.py:121
  2424.7 100.8 %all-gather.29.cloned.1.call-done = f32[768,9216]{1,0:T(8,128)} async-done(((f32[96,9216]{1,0:T(8,128)}), f32[768,9216]{1,0:T(8,128)}) %all-gather.29.cloned.1.call-update) | async-done | bytes 28311568 | tf_op jit(solution)/shard_map/all_gather | solution.py:121
  2565.1 95.0 %all-gather.31.cloned.1.call-done = f32[768,9216]{1,0:T(8,128)} async-done(((f32[96,9216]{1,0:T(8,128)}), f32[768,9216]{1,0:T(8,128)}) %all-gather.31.cloned.1.call-update) | async-done | bytes 28311568 | tf_op jit(solution)/shard_map/all_gather | solution.py:121
  (211 shorter events, 606.9 us)
Async XLA Ops:
  7.2 355.4 %reduce-scatter.13.cloned.1.call-start = ((), (), s32[]{:S(2)}) async-start(), calls=%async_computation.12 | async-start | bytes 10616832 | tf_op jit(solution)/shard_map/reduce_scatter | solution.py:118
  7.2 17.3 copy-start.7
  42.8 17.3 copy-start.21
  78.2 17.9 copy-start.23
  114.2 17.3 copy-start.26
  149.6 18.2 copy-start.29
  186.0 17.4 copy-start.5
  241.7 25.2 copy-start.31
  241.7 155.5 %reduce-scatter.15.cloned.1.call-start = ((), (), s32[]{:S(2)}) async-start(), calls=%async_computation.13 | async-start | bytes 10616832 | tf_op jit(solution)/shard_map/reduce_scatter | solution.py:118
  280.6 248.6 %reduce-scatter.17.cloned.1.call-start = ((), (), s32[]{:S(2)}) async-start(), calls=%async_computation.14 | async-start | bytes 21233664 | tf_op jit(solution)/shard_map/reduce_scatter | solution.py:118
  295.4 18.3 copy-start.36
  313.7 22.8 copy-start.30
  336.5 14.0 copy-start.14
  397.0 240.9 %reduce-scatter.19.cloned.1.call-start = ((), (), s32[]{:S(2)}) async-start(), calls=%async_computation.15 | async-start | bytes 21233664 | tf_op jit(solution)/shard_map/reduce_scatter | solution.py:118
  399.4 22.9 copy-start.27
  444.6 357.9 %reduce-scatter.21.cloned.1.call-start = ((), (), s32[]{:S(2)}) async-start(), calls=%async_computation.16 | async-start | bytes 31850496 | tf_op jit(solution)/shard_map/reduce_scatter | solution.py:118
  478.0 25.3 copy-start.24
  503.3 13.9 copy-start.15
  529.2 21.2 copy-start.33
  550.4 22.9 copy-start.22
  573.3 14.3 copy-start.16
  637.7 329.9 %reduce-scatter.23.cloned.1.call-start = ((), (), s32[]{:S(2)}) async-start(), calls=%async_computation.17 | async-start | bytes 31850496 | tf_op jit(solution)/shard_map/reduce_scatter | solution.py:118
  640.9 22.9 copy-start.8
  698.7 338.8 %all-gather.13.cloned.1.call-start = ((), (), s32[]{:S(2)}) async-start(), calls=%async_computation.18 | async-start | bytes 5308416 | tf_op jit(solution)/shard_map/all_gather | solution.py:121
  806.7 196.0 %copy-start = (f32[384,2304]{1,0:T(8,128)S(1)}, f32[384,2304]{1,0:T(8,128)}, u32[]{:S(2)}) copy-start(f32[384,2304]{1,0:T(8,128)} %reduce-scatter.21.cloned.1.call-done) | copy-start | bytes 10616836
  1002.4 69.8 %all-gather.15.cloned.1.call-start = ((), (), s32[]{:S(2)}) async-start(), calls=%async_computation.19 | async-start | bytes 5308416 | tf_op jit(solution)/shard_map/all_gather | solution.py:121
  1009.2 118.4 %all-gather.17.cloned.1.call-start = ((), (), s32[]{:S(2)}) async-start(), calls=%async_computation.20 | async-start | bytes 10616832 | tf_op jit(solution)/shard_map/all_gather | solution.py:121
  1011.7 170.5 %all-gather.19.cloned.1.call-start = ((), (), s32[]{:S(2)}) async-start(), calls=%async_computation.21 | async-start | bytes 10616832 | tf_op jit(solution)/shard_map/all_gather | solution.py:121
  1014.1 222.9 %all-gather.21.cloned.1.call-start = ((), (), s32[]{:S(2)}) async-start(), calls=%async_computation.22 | async-start | bytes 10616832 | tf_op jit(solution)/shard_map/all_gather | solution.py:121
  1016.6 275.1 %all-gather.23.cloned.1.call-start = ((), (), s32[]{:S(2)}) async-start(), calls=%async_computation.23 | async-start | bytes 10616832 | tf_op jit(solution)/shard_map/all_gather | solution.py:121
  1017.8 323.8 %all-gather.25.cloned.1.call-start = ((), (), s32[]{:S(2)}) async-start(), calls=%async_computation.24 | async-start | bytes 5308416 | tf_op jit(solution)/shard_map/all_gather | solution.py:121
  1018.6 342.6 %all-gather.27.cloned.1.call-start = ((), (), s32[]{:S(2)}) async-start(), calls=%async_computation.25 | async-start | bytes 5308416 | tf_op jit(solution)/shard_map/all_gather | solution.py:121
  1019.1 53.1 %copy-start.9 = (bf16[3,576,768]{2,1,0:T(8,128)(2,1)S(1)}, bf16[3,576,768]{2,1,0:T(8,128)(2,1)}, u32[]{:S(2)}) copy-start(bf16[3,576,768]{2,1,0:T(8,128)(2,1)} %param.4) | copy-start | bytes 7962628
  1019.1 499.4 %reduce-scatter.27.cloned.1.call-start = ((), (), s32[]{:S(2)}) async-start(), calls=%async_computation.27 | async-start | bytes 10616832 | tf_op jit(solution)/shard_map/reduce_scatter | solution.py:118
  1089.1 93.2 %copy-start.19 = (bf16[1728,768]{1,0:T(8,128)(2,1)S(1)}, bf16[1728,768]{1,0:T(8,128)(2,1)}, u32[]{:S(2)}) copy-start(bf16[1728,768]{1,0:T(8,128)(2,1)} %fusion.145) | copy-start | bytes 7962628
  1199.0 16.6 copy-start.20
  1232.4 59.3 %copy-start.25 = (bf16[1728,768]{1,0:T(8,128)(2,1)S(1)}, bf16[1728,768]{1,0:T(8,128)(2,1)}, u32[]{:S(2)}) copy-start(bf16[1728,768]{1,0:T(8,128)(2,1)} %add_convert_fusion.8) | copy-start | bytes 7962628
  1308.5 16.3 copy-start.28
  1341.6 19.5 copy-start.6
  1399.0 152.7 %reduce-scatter.25.cloned.1.call-start = ((), (), s32[]{:S(2)}) async-start(), calls=%async_computation.26 | async-start | bytes 10616832 | tf_op jit(solution)/shard_map/reduce_scatter | solution.py:118
  1436.0 243.6 %reduce-scatter.29.cloned.1.call-start = ((), (), s32[]{:S(2)}) async-start(), calls=%async_computation.28 | async-start | bytes 21233664 | tf_op jit(solution)/shard_map/reduce_scatter | solution.py:118
  1451.0 56.4 %slice-start.6 = ((s8[9437184]{0:T(1024)(128)(4,1)}), s8[1048576]{0:T(1024)(128)(4,1)S(1)}, s32[]{:S(2)}) async-start(s8[9437184]{0:T(1024)(128)(4,1)} %bitcast.263), calls=%async_computation.42 | async-start | bytes 2097152
  1468.5 38.9 %slice-start.7 = ((s8[9437184]{0:T(1024)(128)(4,1)}), s8[4194304]{0:T(1024)(128)(4,1)S(1)}, s32[]{:S(2)}) async-start(s8[9437184]{0:T(1024)(128)(4,1)} %bitcast.263), calls=%async_computation.43 | async-start | bytes 8388608
  1468.5 38.9 %slice-start.8 = ((s8[9437184]{0:T(1024)(128)(4,1)}), s8[4194304]{0:T(1024)(128)(4,1)S(1)}, s32[]{:S(2)}) async-start(s8[9437184]{0:T(1024)(128)(4,1)} %bitcast.263), calls=%async_computation.44 | async-start | bytes 8388608
  1492.6 14.8 copy-start.17
  1551.6 237.7 %reduce-scatter.31.cloned.1.call-start = ((), (), s32[]{:S(2)}) async-start(), calls=%async_computation.29 | async-start | bytes 21233664 | tf_op jit(solution)/shard_map/reduce_scatter | solution.py:118
  1572.3 13.0 copy-start.11
  1596.0 358.6 %reduce-scatter.35.cloned.1.call-start = ((), (), s32[]{:S(2)}) async-start(), calls=%async_computation.33 | async-start | bytes 31850496 | tf_op jit(solution)/shard_map/reduce_scatter | solution.py:118
  1611.9 56.5 %slice-start = ((s8[9437184]{0:T(1024)(128)(4,1)}), s8[1048576]{0:T(1024)(128)(4,1)S(1)}, s32[]{:S(2)}) async-start(s8[9437184]{0:T(1024)(128)(4,1)} %bitcast.259), calls=%async_computation.36 | async-start | bytes 2097152
  1629.5 38.9 %slice-start.1 = ((s8[9437184]{0:T(1024)(128)(4,1)}), s8[4194304]{0:T(1024)(128)(4,1)S(1)}, s32[]{:S(2)}) async-start(s8[9437184]{0:T(1024)(128)(4,1)} %bitcast.259), calls=%async_computation.37 | async-start | bytes 8388608
  1629.5 38.9 %slice-start.2 = ((s8[9437184]{0:T(1024)(128)(4,1)}), s8[4194304]{0:T(1024)(128)(4,1)S(1)}, s32[]{:S(2)}) async-start(s8[9437184]{0:T(1024)(128)(4,1)} %bitcast.259), calls=%async_computation.38 | async-start | bytes 8388608
  1653.6 14.9 copy-start.18
  1679.5 57.3 %slice-start.3 = ((s8[9437184]{0:T(1024)(128)(4,1)}), s8[1048576]{0:T(1024)(128)(4,1)S(1)}, s32[]{:S(2)}) async-start(s8[9437184]{0:T(1024)(128)(4,1)} %bitcast.261), calls=%async_computation.39 | async-start | bytes 2097152
  1697.5 39.3 %slice-start.4 = ((s8[9437184]{0:T(1024)(128)(4,1)}), s8[4194304]{0:T(1024)(128)(4,1)S(1)}, s32[]{:S(2)}) async-start(s8[9437184]{0:T(1024)(128)(4,1)} %bitcast.261), calls=%async_computation.40 | async-start | bytes 8388608
  1697.5 39.3 %slice-start.5 = ((s8[9437184]{0:T(1024)(128)(4,1)}), s8[4194304]{0:T(1024)(128)(4,1)S(1)}, s32[]{:S(2)}) async-start(s8[9437184]{0:T(1024)(128)(4,1)} %bitcast.261), calls=%async_computation.41 | async-start | bytes 8388608
  1722.1 14.7 copy-start.13
  1786.8 26.5 copy-start.10
  1786.9 332.7 %reduce-scatter.33.cloned.1.call-start = ((), (), s32[]{:S(2)}) async-start(), calls=%async_computation.30 | async-start | bytes 31850496 | tf_op jit(solution)/shard_map/reduce_scatter | solution.py:118
  1848.1 271.5 %copy-start.1 = (f32[96,6144]{1,0:T(8,128)S(1)}, f32[96,6144]{1,0:T(8,128)}, u32[]{:S(2)}) copy-start(f32[96,6144]{1,0:T(8,128)} %reduce-scatter.31.cloned.1.call-done) | copy-start | bytes 7077892
  1848.1 271.5 %copy-start.4 = (f32[96,3072]{1,0:T(8,128)S(1)}, f32[96,3072]{1,0:T(8,128)}, u32[]{:S(2)}) copy-start(f32[96,3072]{1,0:T(8,128)} %reduce-scatter.25.cloned.1.call-done) | copy-start | bytes 3538948
  1848.2 407.1 %all-gather.33.cloned.1.call-start = ((), (), s32[]{:S(2)}) async-start(), calls=%async_computation.34 | async-start | bytes 31850496 | tf_op jit(solution)/shard_map/all_gather | solution.py:121
  1954.5 436.1 %all-gather.35.cloned.1.call-start = ((), (), s32[]{:S(2)}) async-start(), calls=%async_computation.35 | async-start | bytes 31850496 | tf_op jit(solution)/shard_map/all_gather | solution.py:121
  1958.6 566.9 %all-gather.29.cloned.1.call-start = ((), (), s32[]{:S(2)}) async-start(), calls=%async_computation.31 | async-start | bytes 31850496 | tf_op jit(solution)/shard_map/all_gather | solution.py:121
  2119.6 540.6 %all-gather.31.cloned.1.call-start = ((), (), s32[]{:S(2)}) async-start(), calls=%async_computation.32 | async-start | bytes 31850496 | tf_op jit(solution)/shard_map/all_gather | solution.py:121
  (7 other events, 25.2 us)
Sparse Core Ops, SparseCore 0:
  241.8 70.2 reduce-scatter.12
  315.5 67.3 reduce-scatter.14
  397.1 119.8 reduce-scatter.16
  520.4 117.0 reduce-scatter.18
  641.5 160.9 reduce-scatter.20
  806.5 160.9 reduce-scatter.22
  1002.6 34.8 all-gather.12
  1039.3 32.9 all-gather.14
  1074.6 52.9 all-gather.16
  1129.3 52.9 all-gather.18
  1184.1 52.9 all-gather.20
  1238.7 52.9 all-gather.22
  1293.5 32.9 all-gather.24
  1328.1 32.9 all-gather.26
  1399.1 67.4 reduce-scatter.26
  1469.8 67.4 reduce-scatter.24
  1551.8 117.0 reduce-scatter.28
  1672.2 117.0 reduce-scatter.30
  1793.5 160.9 reduce-scatter.34
  1958.5 160.9 reduce-scatter.32
  2121.4 133.8 all-gather.32
  2257.7 132.9 all-gather.34
  2392.5 132.9 all-gather.28
  2527.2 132.9 all-gather.30

commit v3 on v2

--- a/solution.py
+++ b/solution.py
@@ -153,9 +153,12 @@
         second = per_layer(backward(d_pert, saved_pert, pert_in, pert_out, scatter, lambda kind, members, shard: shard, groups), width)
         loss_total = lax.psum(loss_local, mesh_axes)
         full = {}
-        for members in ((5, 4, 3), (2, 1, 0)):
-            for kind in ('out', 'in'):
-                full.update(gather_layers(kind, members, [second[kind, layer_idx] for layer_idx in members]))
+        down = tuple(reversed(range(layers)))
+        all_out = gather(row_major(jnp.concatenate([second['out', layer_idx] for layer_idx in down], axis=1)))
+        most_in = gather(row_major(jnp.concatenate([second['in', layer_idx] for layer_idx in down[:-1]], axis=1)))
+        all_out, most_in, last_in = lax.optimization_barrier((all_out, most_in, second['in', 0]))
+        full.update(per_layer({('out', down): all_out, ('in', down[:-1]): most_in}, width))
+        full.update(gather_layers('in', (0,), [last_in]))
         new_in = [w_in[layer_idx] - LEARN_RATE * full['in', layer_idx] for layer_idx in range(layers)]
         new_out = [w_out[layer_idx] - LEARN_RATE * full['out', layer_idx] for layer_idx in range(layers)]
         return jnp.stack(new_in), jnp.stack(new_out), loss_total * inv_count

time: 2720 us -> 2830 us (1.040)
  waiting for transfers between devices: 1100 us -> 1210 us
    all_gather x12 -> x11, waiting for transfers between devices: 568 us -> 625 us  [gather(): return lax.all_gather(shard, mesh_axes, axis=0, tiled=True)]
    reduce_scatter x12, waiting for transfers between devices: 532 us -> 584 us  [scatter(): lax.psum_scatter(grad, mesh_axes, scatter_dimension=0, tiled=True)]
  transfers between devices with their start and end apart: 24 -> 23, of which waited for: 16 -> 14; matrix products, arithmetic and copies ran while one was open for 44% -> 39% of each run, Pallas kernels for 0% -> 0%
where the time goes in v3:
time: 2830 us; the launch traced here: 2820 us
  waiting for transfers between devices  1210 us (43%)
  matrix products  1200 us (42%)
  other arithmetic  333 us (12%)
  blocking collectives  45.4 us (2%)
    all_gather x11, waiting for transfers between devices, gather(): return lax.all_gather(shard, mesh_axes, axis=0, tiled=True)  625 us
    reduce_scatter x12, waiting for transfers between devices, scatter(): lax.psum_scatter(grad, mesh_axes, scatter_dimension=0, tiled=True)  584 us
    dot_general x12, matrix products, backward(): jnp.einsum('td,fd->tf', d_hidden, out_list[layer_idx], preferred_element_...  279 us
    dot_general x12, matrix products, forward(): jnp.dot(post_act, out_list[layer_idx], preferred_element_type=jnp.float32)  215 us
    dot_general x12, matrix products, backward(): jnp.einsum('tf,td->fd', post_act, d_hidden, preferred_element_type=jnp.fl...  212 us
    dot_general x12, matrix products, forward(): jnp.dot(hidden, in_list[layer_idx], preferred_element_type=jnp.float32)  202 us
    dot_general x12, matrix products, backward(): jnp.einsum('td,tf->df', hidden, d_pre, preferred_element_type=jnp.float32)  166 us
    concatenate x8, other arithmetic, launch(): jnp.concatenate(parts, axis=1)  135 us
  transfers between devices with their start and end apart: 23, of which 14 were waited for; matrix products, arithmetic and copies ran while one was open for 39% of the time, Pallas kernels for 0%

profile of v3, /device:TPU:0, one launch (start us, length us, event | category | flops | bytes accessed | tf_op | source)
XLA Modules:
  0.0 2824.5 jit_solution(9170828904978381303)
XLA Ops:
  7.2 17.3 fusion.8
  24.5 18.2 fusion.108
  42.7 17.3 fusion.17
  60.0 18.1 add_convert_fusion.19
  78.2 18.1 fusion.26
  96.3 18.1 add_convert_fusion.18
  114.4 17.4 fusion.35
  131.8 18.1 add_convert_fusion.17
  149.9 18.1 fusion.44
  168.0 18.2 add_convert_fusion.16
  186.2 17.5 fusion.53
  203.7 20.1 fusion.111
  223.8 18.1 fusion.190
  242.0 25.2 fusion.57
  295.7 18.3 fusion.193
  314.0 22.8 fusion.48
  365.1 17.1 fusion.196
  399.8 22.9 fusion.39
  460.8 17.5 fusion.199
  478.3 25.3 fusion.30
  533.4 17.3 fusion.202
  550.6 22.9 fusion.21
  599.9 17.1 fusion.205
  617.0 20.9 pad_maximum_fusion
  641.1 22.9 fusion.12
  677.9 21.1 pad_maximum_fusion.1
  701.6 101.2 %reduce-scatter.21.cloned.1.call-done = f32[384,2304]{1,0:T(8,128)} async-done(((f32[3072,2304]{1,0:T(8,128)}), f32[384,2304]{1,0:T(8,128)}) %reduce-scatter.21.cloned.1.call-update) | async-done | bytes 3538960 | tf_op jit(solution)/shard_map/reduce_scatter | solution.py:118
  807.0 160.8 %reduce-scatter.23.cloned.1.call-done = f32[96,9216]{1,0:T(8,128)} async-done(((f32[768,9216]{1,0:T(8,128)}), f32[96,9216]{1,0:T(8,128)}) %reduce-scatter.23.cloned.1.call-update) | async-done | bytes 3538960 | tf_op jit(solution)/shard_map/reduce_scatter | solution.py:118
  972.0 22.2 psum.14
  1019.5 18.2 all-gather.12.cloned.1.call-done
  1053.6 18.9 all-gather.14.cloned.1.call-done
  1072.6 16.9 fusion.109
  1089.4 38.5 %all-gather.16.cloned.1.call-done = bf16[768,6144]{1,0:T(8,128)(2,1)} async-done(((bf16[96,6144]{1,0:T(8,128)(2,1)}), bf16[768,6144]{1,0:T(8,128)(2,1)}) %all-gather.16.cloned.1.call-update) | async-done | bytes 9437200 | tf_op jit(solution)/shard_map/all_gather | solution.py:121
  1143.8 38.8 %all-gather.18.cloned.1.call-done = bf16[3072,1536]{1,0:T(8,128)(2,1)} async-done(((bf16[384,1536]{1,0:T(8,128)(2,1)}), bf16[3072,1536]{1,0:T(8,128)(2,1)}) %all-gather.18.cloned.1.call-update) | async-done | bytes 9437200 | tf_op jit(solution)/shard_map/all_gather | solution.py:121
  1182.6 16.8 add_convert_fusion.9
  1199.3 16.5 fusion.71
  1215.9 16.8 add_convert_fusion.8
  1237.3 16.0 fusion.80
  1253.3 38.7 %all-gather.22.cloned.1.call-done = bf16[3072,1536]{1,0:T(8,128)(2,1)} async-done(((bf16[384,1536]{1,0:T(8,128)(2,1)}), bf16[3072,1536]{1,0:T(8,128)(2,1)}) %all-gather.22.cloned.1.call-update) | async-done | bytes 9437200 | tf_op jit(solution)/shard_map/all_gather | solution.py:121
  1292.0 16.8 add_convert_fusion.7
  1308.7 16.4 fusion.89
  1325.2 16.9 add_convert_fusion.6
  1342.0 16.2 fusion.98
  1361.4 19.8 multiply_reduce_fusion
  1381.2 18.1 fusion.175
  1399.4 19.7 fusion.102
  1451.3 17.5 fusion.178
  1468.8 24.1 fusion.93
  1518.9 17.9 fusion.181
  1551.9 20.8 fusion.84
  1612.3 17.6 fusion.184
  1629.9 24.1 fusion.75
  1679.9 17.9 fusion.187
  1697.8 24.7 fusion.66
  1748.2 18.0 fusion.172
  1766.3 23.2 reduce-scatter.33.cloned.1.call-done
  1789.5 23.8 fusion.4
  1827.1 21.1 pad_maximum_fusion.3
  1848.2 20.9 pad_maximum_fusion.2
  1869.2 140.1 %reduce-scatter.35.cloned.1.call-done = f32[96,9216]{1,0:T(8,128)} async-done(((f32[768,9216]{1,0:T(8,128)}), f32[96,9216]{1,0:T(8,128)}) %reduce-scatter.35.cloned.1.call-update) | async-done | bytes 3538960 | tf_op jit(solution)/shard_map/reduce_scatter | solution.py:118
  2016.1 158.2 %reduce-scatter.31.cloned.1.call-done = f32[384,2304]{1,0:T(8,128)} async-done(((f32[3072,2304]{1,0:T(8,128)}), f32[384,2304]{1,0:T(8,128)}) %reduce-scatter.31.cloned.1.call-update) | async-done | bytes 3538960 | tf_op jit(solution)/shard_map/reduce_scatter | solution.py:118
  2181.5 208.2 %all-gather.30.cloned.1.call-done = f32[768,15360]{1,0:T(8,128)} async-done(((f32[96,15360]{1,0:T(8,128)}), f32[768,15360]{1,0:T(8,128)}) %all-gather.30.cloned.1.call-update) | async-done | bytes 47185936 | tf_op jit(solution)/shard_map/all_gather | solution.py:121
  2389.7 255.4 %all-gather.28.cloned.1.call-done = f32[3072,4608]{1,0:T(8,128)} async-done(((f32[384,4608]{1,0:T(8,128)}), f32[3072,4608]{1,0:T(8,128)}) %all-gather.28.cloned.1.call-update) | async-done | bytes 56623120 | tf_op jit(solution)/shard_map/all_gather | solution.py:121
  2645.7 23.1 psum.15
  (210 shorter events, 596.3 us)
Async XLA Ops:
  7.2 355.7 %reduce-scatter.13.cloned.1.call-start = ((), (), s32[]{:S(2)}) async-start(), calls=%async_computation.12 | async-start | bytes 10616832 | tf_op jit(solution)/shard_map/reduce_scatter | solution.py:118
  7.2 17.3 copy-start.7
  42.7 17.3 copy-start.21
  78.2 18.1 copy-start.23
  114.4 17.4 copy-start.26
  149.9 18.1 copy-start.29
  186.2 17.5 copy-start.5
  241.9 25.2 copy-start.31
  241.9 155.6 %reduce-scatter.15.cloned.1.call-start = ((), (), s32[]{:S(2)}) async-start(), calls=%async_computation.13 | async-start | bytes 10616832 | tf_op jit(solution)/shard_map/reduce_scatter | solution.py:118
  280.9 248.6 %reduce-scatter.17.cloned.1.call-start = ((), (), s32[]{:S(2)}) async-start(), calls=%async_computation.14 | async-start | bytes 21233664 | tf_op jit(solution)/shard_map/reduce_scatter | solution.py:118
  295.7 18.3 copy-start.36
  314.0 22.8 copy-start.30
  336.8 14.1 copy-start.14
  397.3 240.9 %reduce-scatter.19.cloned.1.call-start = ((), (), s32[]{:S(2)}) async-start(), calls=%async_computation.15 | async-start | bytes 21233664 | tf_op jit(solution)/shard_map/reduce_scatter | solution.py:118
  399.8 22.9 copy-start.27
  444.9 357.9 %reduce-scatter.21.cloned.1.call-start = ((), (), s32[]{:S(2)}) async-start(), calls=%async_computation.16 | async-start | bytes 31850496 | tf_op jit(solution)/shard_map/reduce_scatter | solution.py:118
  478.3 25.3 copy-start.24
  503.6 13.9 copy-start.15
  529.5 21.2 copy-start.33
  550.6 22.9 copy-start.22
  573.6 14.3 copy-start.16
  637.9 330.0 %reduce-scatter.23.cloned.1.call-start = ((), (), s32[]{:S(2)}) async-start(), calls=%async_computation.17 | async-start | bytes 31850496 | tf_op jit(solution)/shard_map/reduce_scatter | solution.py:118
  641.1 22.9 copy-start.8
  699.0 338.8 %all-gather.12.cloned.1.call-start = ((), (), s32[]{:S(2)}) async-start(), calls=%async_computation.18 | async-start | bytes 5308416 | tf_op jit(solution)/shard_map/all_gather | solution.py:121
  807.0 196.0 %copy-start = (f32[384,2304]{1,0:T(8,128)S(1)}, f32[384,2304]{1,0:T(8,128)}, u32[]{:S(2)}) copy-start(f32[384,2304]{1,0:T(8,128)} %reduce-scatter.21.cloned.1.call-done) | copy-start | bytes 10616836
  1002.8 69.8 %all-gather.14.cloned.1.call-start = ((), (), s32[]{:S(2)}) async-start(), calls=%async_computation.19 | async-start | bytes 5308416 | tf_op jit(solution)/shard_map/all_gather | solution.py:121
  1009.5 7.5 copy-start.3
  1009.6 118.3 %all-gather.16.cloned.1.call-start = ((), (), s32[]{:S(2)}) async-start(), calls=%async_computation.20 | async-start | bytes 10616832 | tf_op jit(solution)/shard_map/all_gather | solution.py:121
  1012.1 170.5 %all-gather.18.cloned.1.call-start = ((), (), s32[]{:S(2)}) async-start(), calls=%async_computation.21 | async-start | bytes 10616832 | tf_op jit(solution)/shard_map/all_gather | solution.py:121
  1014.5 222.8 %all-gather.20.cloned.1.call-start = ((), (), s32[]{:S(2)}) async-start(), calls=%async_computation.22 | async-start | bytes 10616832 | tf_op jit(solution)/shard_map/all_gather | solution.py:121
  1017.0 275.0 %all-gather.22.cloned.1.call-start = ((), (), s32[]{:S(2)}) async-start(), calls=%async_computation.23 | async-start | bytes 10616832 | tf_op jit(solution)/shard_map/all_gather | solution.py:121
  1018.2 323.9 %all-gather.24.cloned.1.call-start = ((), (), s32[]{:S(2)}) async-start(), calls=%async_computation.24 | async-start | bytes 5308416 | tf_op jit(solution)/shard_map/all_gather | solution.py:121
  1018.9 342.5 %all-gather.26.cloned.1.call-start = ((), (), s32[]{:S(2)}) async-start(), calls=%async_computation.25 | async-start | bytes 5308416 | tf_op jit(solution)/shard_map/all_gather | solution.py:121
  1019.5 53.1 %copy-start.9 = (bf16[3,576,768]{2,1,0:T(8,128)(2,1)S(1)}, bf16[3,576,768]{2,1,0:T(8,128)(2,1)}, u32[]{:S(2)}) copy-start(bf16[3,576,768]{2,1,0:T(8,128)(2,1)} %param.4) | copy-start | bytes 7962628
  1019.5 499.4 %reduce-scatter.25.cloned.1.call-start = ((), (), s32[]{:S(2)}) async-start(), calls=%async_computation.26 | async-start | bytes 10616832 | tf_op jit(solution)/shard_map/reduce_scatter | solution.py:118
  1089.4 93.1 %copy-start.19 = (bf16[1728,768]{1,0:T(8,128)(2,1)S(1)}, bf16[1728,768]{1,0:T(8,128)(2,1)}, u32[]{:S(2)}) copy-start(bf16[1728,768]{1,0:T(8,128)(2,1)} %fusion.109) | copy-start | bytes 7962628
  1199.3 16.5 copy-start.20
  1232.6 59.4 %copy-start.25 = (bf16[1728,768]{1,0:T(8,128)(2,1)S(1)}, bf16[1728,768]{1,0:T(8,128)(2,1)}, u32[]{:S(2)}) copy-start(bf16[1728,768]{1,0:T(8,128)(2,1)} %add_convert_fusion.8) | copy-start | bytes 7962628
  1308.7 16.4 copy-start.28
  1342.0 19.4 copy-start.6
  1399.4 152.5 %reduce-scatter.29.cloned.1.call-start = ((), (), s32[]{:S(2)}) async-start(), calls=%async_computation.28 | async-start | bytes 10616832 | tf_op jit(solution)/shard_map/reduce_scatter | solution.py:118
  1436.2 243.7 %reduce-scatter.27.cloned.1.call-start = ((), (), s32[]{:S(2)}) async-start(), calls=%async_computation.27 | async-start | bytes 21233664 | tf_op jit(solution)/shard_map/reduce_scatter | solution.py:118
  1451.3 56.5 %slice-start.6 = ((s8[9437184]{0:T(1024)(128)(4,1)}), s8[1048576]{0:T(1024)(128)(4,1)S(1)}, s32[]{:S(2)}) async-start(s8[9437184]{0:T(1024)(128)(4,1)} %bitcast.263), calls=%async_computation.41 | async-start | bytes 2097152
  1468.8 39.0 %slice-start.7 = ((s8[9437184]{0:T(1024)(128)(4,1)}), s8[4194304]{0:T(1024)(128)(4,1)S(1)}, s32[]{:S(2)}) async-start(s8[9437184]{0:T(1024)(128)(4,1)} %bitcast.263), calls=%async_computation.42 | async-start | bytes 8388608
  1468.8 39.0 %slice-start.8 = ((s8[9437184]{0:T(1024)(128)(4,1)}), s8[4194304]{0:T(1024)(128)(4,1)S(1)}, s32[]{:S(2)}) async-start(s8[9437184]{0:T(1024)(128)(4,1)} %bitcast.263), calls=%async_computation.43 | async-start | bytes 8388608
  1492.9 14.9 copy-start.17
  1551.8 237.7 %reduce-scatter.33.cloned.1.call-start = ((), (), s32[]{:S(2)}) async-start(), calls=%async_computation.31 | async-start | bytes 21233664 | tf_op jit(solution)/shard_map/reduce_scatter | solution.py:118
  1572.7 13.0 copy-start.11
  1596.3 412.9 %reduce-scatter.35.cloned.1.call-start = ((), (), s32[]{:S(2)}) async-start(), calls=%async_computation.32 | async-start | bytes 31850496 | tf_op jit(solution)/shard_map/reduce_scatter | solution.py:118
  1612.3 56.5 %slice-start = ((s8[9437184]{0:T(1024)(128)(4,1)}), s8[1048576]{0:T(1024)(128)(4,1)S(1)}, s32[]{:S(2)}) async-start(s8[9437184]{0:T(1024)(128)(4,1)} %bitcast.259), calls=%async_computation.35 | async-start | bytes 2097152
  1629.9 38.9 %slice-start.1 = ((s8[9437184]{0:T(1024)(128)(4,1)}), s8[4194304]{0:T(1024)(128)(4,1)S(1)}, s32[]{:S(2)}) async-start(s8[9437184]{0:T(1024)(128)(4,1)} %bitcast.259), calls=%async_computation.36 | async-start | bytes 8388608
  1629.9 38.9 %slice-start.2 = ((s8[9437184]{0:T(1024)(128)(4,1)}), s8[4194304]{0:T(1024)(128)(4,1)S(1)}, s32[]{:S(2)}) async-start(s8[9437184]{0:T(1024)(128)(4,1)} %bitcast.259), calls=%async_computation.37 | async-start | bytes 8388608
  1654.0 14.9 copy-start.18
  1679.9 57.2 %slice-start.3 = ((s8[9437184]{0:T(1024)(128)(4,1)}), s8[1048576]{0:T(1024)(128)(4,1)S(1)}, s32[]{:S(2)}) async-start(s8[9437184]{0:T(1024)(128)(4,1)} %bitcast.261), calls=%async_computation.38 | async-start | bytes 2097152
  1697.8 39.3 %slice-start.4 = ((s8[9437184]{0:T(1024)(128)(4,1)}), s8[4194304]{0:T(1024)(128)(4,1)S(1)}, s32[]{:S(2)}) async-start(s8[9437184]{0:T(1024)(128)(4,1)} %bitcast.261), calls=%async_computation.39 | async-start | bytes 8388608
  1697.8 39.3 %slice-start.5 = ((s8[9437184]{0:T(1024)(128)(4,1)}), s8[4194304]{0:T(1024)(128)(4,1)S(1)}, s32[]{:S(2)}) async-start(s8[9437184]{0:T(1024)(128)(4,1)} %bitcast.261), calls=%async_computation.40 | async-start | bytes 8388608
  1722.5 14.7 copy-start.13
  1766.3 47.1 %copy-start.10 = (bf16[3,576,768]{2,1,0:T(8,128)(2,1)S(1)}, bf16[3,576,768]{2,1,0:T(8,128)(2,1)}, u32[]{:S(2)}) copy-start(bf16[3,576,768]{2,1,0:T(8,128)(2,1)} %param.4) | copy-start | bytes 7962628
  1848.2 326.2 %reduce-scatter.31.cloned.1.call-start = ((), (), s32[]{:S(2)}) async-start(), calls=%async_computation.29 | async-start | bytes 31850496 | tf_op jit(solution)/shard_map/reduce_scatter | solution.py:118
  1869.1 305.2 %copy-start.1 = (f32[384,1536]{1,0:T(8,128)S(1)}, f32[384,1536]{1,0:T(8,128)}, u32[]{:S(2)}) copy-start(f32[384,1536]{1,0:T(8,128)} %reduce-scatter.27.cloned.1.call-done) | copy-start | bytes 7077892
  1869.1 305.2 %copy-start.4 = (f32[384,768]{1,0:T(8,128)S(1)}, f32[384,768]{1,0:T(8,128)}, u32[]{:S(2)}) copy-start(f32[384,768]{1,0:T(8,128)} %reduce-scatter.25.cloned.1.call-done) | copy-start | bytes 3538948
  1869.1 520.6 %all-gather.30.cloned.1.call-start = ((), (), s32[]{:S(2)}) async-start(), calls=%async_computation.33 | async-start | bytes 53084160 | tf_op jit(solution)/shard_map/all_gather | solution.py:121
  2016.1 629.0 %all-gather.28.cloned.1.call-start = ((), (), s32[]{:S(2)}) async-start(), calls=%async_computation.30 | async-start | bytes 63700992 | tf_op jit(solution)/shard_map/all_gather | solution.py:121
  2179.1 558.6 %all-gather.32.cloned.1.call-start = ((), (), s32[]{:S(2)}) async-start(), calls=%async_computation.34 | async-start | bytes 10616832 | tf_op jit(solution)/shard_map/all_gather | solution.py:121
  (6 other events, 17.7 us)
Sparse Core Ops, SparseCore 0:
  242.0 70.2 reduce-scatter.12
  315.7 67.4 reduce-scatter.14
  397.4 119.8 reduce-scatter.16
  520.7 117.0 reduce-scatter.18
  641.8 160.9 reduce-scatter.20
  806.9 160.9 reduce-scatter.22
  1002.9 34.8 all-gather.11
  1039.6 32.9 all-gather.13
  1074.9 52.9 all-gather.15
  1129.6 52.9 all-gather.17
  1184.4 52.9 all-gather.19
  1239.0 52.9 all-gather.21
  1293.8 32.9 all-gather.23
  1328.4 32.9 all-gather.25
  1399.5 67.4 reduce-scatter.24
  1470.2 67.4 reduce-scatter.28
  1552.0 117.0 reduce-scatter.26
  1672.4 117.0 reduce-scatter.32
  1848.3 160.9 reduce-scatter.34
  2013.3 160.9 reduce-scatter.30
  2176.2 213.4 all-gather.29
  2392.1 252.9 all-gather.27
  2647.4 53.8 all-gather.31
